TPU v7x, 128 devices: a whole 4x4x4 slice. The times are simulated.
128 devices in a mesh: rows: 16 (over z_hi, x, core), cols: 8 (over y, z_lo).
Axes of the slice: x: 4, y: 4, z: 4 (z_hi: 2, z_lo: 2; z = z_hi * 2 + z_lo), core: 2. Of those that a mesh axis runs over, the one named last changes fastest.
Arguments:
- block_values: bfloat16 [65536, 128], P(('rows', 'cols')), may hold values from -6 to 6
- block_length: int32 [65536], P(('rows', 'cols')), may hold values from 1 to 128
- block_owner: int32 [65536], P(('rows', 'cols')), may hold values from 0 to 16383, as said below
- block_second: int32 [65536], P(('rows', 'cols')), may hold values from 0 to 16383, as said below
- block_third: int32 [65536, 128], P(('rows', 'cols')), may hold values from 0 to 32767
- live_blocks: int32 [128], P(('rows', 'cols')), may hold values from 1 to 512, as said below
- second_factor: bfloat16 [16384, 256], P('cols', 'rows')
- third_factor: bfloat16 [32768, 256], P('cols', 'rows'), may hold values from -6 to 6
Outputs:
- first_factor: float32 [16384, 256], P('cols', 'rows')
Inputs may be any that keep to these rules, and one draw needn't show every extreme that they name: `block_owner`: slot b lies on device d = b // 512 with index r along rows; its row lies in r * 16384 // 16 up to (r + 1) * 16384 // 16 - 1, the device's mode-1 slab. `block_second`: slot b lies on device d = b // 512 with index c along cols; its row lies in c * 16384 // 8 up to (c + 1) * 16384 // 8 - 1. `live_blocks`: some device uses all 512 slots in every draw.
All inputs are finite; a program needn't handle non-finite values.
Results may differ from a plain program's by a relative error of at most 0.0003.
Values may be sent and summed in bfloat16 or wider, within the bound.
A program may use at most 128 MiB of HBM per device.

v0:
```python
import jax
import jax.numpy as jnp
from jax import lax
from jax.sharding import PartitionSpec as P

I_DEV = 128


def joined_along(blocks, dim):
    shape = list(blocks.shape[1:])
    shape[dim] *= blocks.shape[0]
    return jnp.moveaxis(blocks, 0, dim).reshape(shape)


def from_everyone(value, axis):
    size = lax.axis_size(axis)
    return lax.all_to_all(
        jnp.broadcast_to(value[None], (size, *value.shape)), axis, 0, 0, tiled=True
    )


def collect(value, axis, dim):
    return joined_along(from_everyone(value, axis), dim)


def gram_product(left, right):
    contract = (((0,), (0,)), ((), ()))
    return lax.dot_general(left, right, contract, preferred_element_type=jnp.float32)


def block_fold(values, third, table):
    group = values.shape[0]
    width = values.shape[1]
    picked = table[third.reshape(group * width)]
    scaled = values.reshape(group * width, 1).astype(jnp.float32) * picked.astype(jnp.float32)
    return jnp.sum(scaled.reshape(group, width, picked.shape[1]), axis=1)


def per_device(
    block_values,
    block_length,
    block_owner,
    block_second,
    block_third,
    live_blocks,
    second_factor,
    third_factor,
):
    n_rows = lax.axis_size("rows")
    n_cols = lax.axis_size("cols")
    row_at = lax.axis_index("rows")
    col_at = lax.axis_index("cols")
    contract = (((0,), (0,)), ((), ()))
    width = block_values.shape[1]
    lane = jnp.arange(width, dtype=jnp.int32)
    slab = I_DEV * n_cols
    owned = jnp.arange(slab, dtype=jnp.int32)
    second_range = lax.all_gather(second_factor, "rows", axis=1, tiled=True)
    third_part = collect(third_factor, "cols", 0)
    third_whole = lax.all_gather(third_part, "rows", axis=1, tiled=True)
    range_rows = second_range.shape[0]
    local_gram = gram_product(second_range, second_range)
    gram_second = lax.psum(local_gram, "cols") / (range_rows * n_cols)
    gram_third = gram_product(third_whole, third_whole) / third_whole.shape[0]
    gram = gram_second * gram_third
    nblk = block_values.shape[0]
    group = min(nblk, 128)
    count = live_blocks[0]

    def accumulate(step, total):
        start = step * group
        values = lax.dynamic_slice_in_dim(block_values, start, group, 0)
        lengths = lax.dynamic_slice_in_dim(block_length, start, group, 0)
        third = lax.dynamic_slice_in_dim(block_third, start, group, 0)
        second = lax.dynamic_slice_in_dim(block_second, start, group, 0)
        owner = lax.dynamic_slice_in_dim(block_owner, start, group, 0)
        slot = start + jnp.arange(group, dtype=jnp.int32)
        live = (lane[None, :] < lengths[:, None]) & (slot < count)[:, None]
        values = jnp.where(live, values, jnp.zeros((), jnp.bfloat16))
        fold = block_fold(values, third, third_whole)
        contrib = second_range[second - col_at * range_rows].astype(jnp.float32) * fold
        onehot = ((owner - row_at * slab)[:, None] == owned[None, :]).astype(jnp.float32)
        return total + lax.dot_general(
            onehot,
            contrib,
            contract,
            precision=lax.Precision.HIGHEST,
            preferred_element_type=jnp.float32,
        )

    start_total = jnp.zeros((slab, gram.shape[0]), jnp.float32)
    partial_rows = lax.fori_loop(0, nblk // group, accumulate, start_total)
    mine = lax.psum_scatter(partial_rows, "cols", scatter_dimension=0, tiled=True)
    factor = jnp.linalg.cholesky(gram)
    solved = jax.scipy.linalg.cho_solve((factor, True), mine.T).T
    moved = lax.all_to_all(
        lax.all_to_all(solved, "rows", split_axis=1, concat_axis=0, tiled=True),
        "cols",
        split_axis=0,
        concat_axis=0,
        tiled=True,
    )
    share = n_rows // n_cols
    owned_rows = mine.shape[0]
    reordered = moved.reshape(n_cols, share, owned_rows, moved.shape[1]).transpose(1, 0, 2, 3)
    return reordered.reshape(n_rows * owned_rows, moved.shape[1])


def solution(mesh):
    return jax.shard_map(
        per_device,
        mesh=mesh,
        in_specs=(
            P(("rows", "cols"), None),
            P(("rows", "cols")),
            P(("rows", "cols")),
            P(("rows", "cols")),
            P(("rows", "cols"), None),
            P(("rows", "cols")),
            P("cols", "rows"),
            P("cols", "rows"),
        ),
        out_specs=P("cols", "rows"),
        check_vma=False,
    )
```

profile of v0, /device:TPU:25, one launch (start us, length us, event | category | flops | bytes accessed | tf_op | source)
XLA Modules:
  0.0 619.5 jit_solution(15795296984549790997)
XLA Ops:
  6.5 0.7 all-gather.3.cloned.1.call-update
  7.3 1.0 broadcast_in_dim.48
  8.3 17.8 %all_to_all.30 = bf16[8,4096,16]{1,2,0:T(8,128)(2,1)S(1)} all-to-all(bf16[8,4096,16]{1,2,0:T(8,128)(2,1)S(1)} %broadcast_in_dim.48), channel_id=1, replica_groups=mesh['rows'=16,'cols'=8] {'cols'}, dimensions={0} | all-to-all | bytes 2097152 | tf_op jit(solution)/shard_map/all_to_all | solution.py:17
  26.1 1.1 copy.51
  27.3 31.9 %all-gather.3.cloned.1.call-done = bf16[2048,256]{0,1:T(8,128)(2,1)} async-done(((bf16[2048,16]{0,1:T(8,128)(2,1)}), bf16[2048,256]{0,1:T(8,128)(2,1)}) %all-gather.3.cloned.1.call-update) | async-done | bytes 1048592 | tf_op jit(solution)/shard_map/all_gather | solution.py:58
  59.3 2.8 fusion.24
  62.1 1.5 copy.43
  63.6 106.6 %all-gather.5.cloned.1.call-done = bf16[32768,256]{0,1:T(8,128)(2,1)} async-done(((bf16[32768,16]{0,1:T(8,128)(2,1)}), bf16[32768,256]{0,1:T(8,128)(2,1)}) %all-gather.5.cloned.1.call-update) | async-done | bytes 16777232 | tf_op jit(solution)/shard_map/all_gather | solution.py:60
  170.2 22.4 %copy.44 = bf16[32768,256]{1,0:T(8,128)(2,1)} copy(bf16[32768,256]{0,1:T(8,128)(2,1)} %all-gather.5.cloned.1.call-done) | data formatting | bytes 33554432
  192.6 321.0 %while.18 = (s32[]{:T(128)}, f32[1024,256]{1,0:T(8,128)S(1)}, s32[512]{0:T(512)}, s32[]{:T(128)}, s32[512]{0:T(512)}, /*index=5*/s32[]{:T(128)}, bf16[2048,256]{...) while((s32[]{:T(128)}, f32[1024,256]{1,0:T(8,128)S(1)}, ...), condition=%wide.region_7.8_spmd.clone, body=%wide.region_5.7_spmd.clone.sunk | while | flops 416057216 | bytes 28354028 | solution.py:92
  192.6 0.8 dynamic_slice.61
  193.4 0.7 add_compare_fusion.2
  194.0 0.9 fusion.42
  194.9 0.9 constant_dynamic-slice_fusion.5
  195.8 68.7 %gather_fusion = bf16[16384,256]{1,0:T(8,128)(2,1)} fusion(bf16[32768,256]{1,0:T(8,128)(2,1)} %get-tuple-element.593, s32[16384]{0:T(1024)S(1)} %broadcast_clamp_fusion.2), kind=kCustom, calls=%fused_computation.1.clone.clone.1 | custom fusion | bytes 16842752 | tf_op jit(solution)/shard_map/while/body/eval_jaxpr/gather | solution.py:34
  264.5 5.5 fusion.43
  270.0 0.8 compare_select_fusion.4
  270.8 0.8 gather_fusion.1
  271.6 1.2 convolution_add_fusion.2
  272.8 0.8 dynamic_slice.61
  273.6 0.7 add_compare_fusion.2
  274.2 0.9 fusion.42
  275.1 0.9 constant_dynamic-slice_fusion.5
  276.1 68.7 %gather_fusion = bf16[16384,256]{1,0:T(8,128)(2,1)} fusion(bf16[32768,256]{1,0:T(8,128)(2,1)} %get-tuple-element.593, s32[16384]{0:T(1024)S(1)} %broadcast_clamp_fusion.2), kind=kCustom, calls=%fused_computation.1.clone.clone.1 | custom fusion | bytes 16842752 | tf_op jit(solution)/shard_map/while/body/eval_jaxpr/gather | solution.py:34
  344.7 5.5 fusion.43
  350.2 0.8 compare_select_fusion.4
  351.0 0.8 gather_fusion.1
  351.8 1.2 convolution_add_fusion.2
  353.0 0.8 dynamic_slice.61
  353.8 0.7 add_compare_fusion.2
  354.4 0.9 fusion.42
  355.3 0.9 constant_dynamic-slice_fusion.5
  356.3 68.7 %gather_fusion = bf16[16384,256]{1,0:T(8,128)(2,1)} fusion(bf16[32768,256]{1,0:T(8,128)(2,1)} %get-tuple-element.593, s32[16384]{0:T(1024)S(1)} %broadcast_clamp_fusion.2), kind=kCustom, calls=%fused_computation.1.clone.clone.1 | custom fusion | bytes 16842752 | tf_op jit(solution)/shard_map/while/body/eval_jaxpr/gather | solution.py:34
  424.9 5.5 fusion.43
  430.4 0.8 compare_select_fusion.4
  431.2 0.8 gather_fusion.1
  432.0 1.2 convolution_add_fusion.2
  433.2 0.8 dynamic_slice.61
  434.0 0.7 add_compare_fusion.2
  434.7 0.9 fusion.42
  435.5 0.9 constant_dynamic-slice_fusion.5
  436.5 68.7 %gather_fusion = bf16[16384,256]{1,0:T(8,128)(2,1)} fusion(bf16[32768,256]{1,0:T(8,128)(2,1)} %get-tuple-element.593, s32[16384]{0:T(1024)S(1)} %broadcast_clamp_fusion.2), kind=kCustom, calls=%fused_computation.1.clone.clone.1 | custom fusion | bytes 16842752 | tf_op jit(solution)/shard_map/while/body/eval_jaxpr/gather | solution.py:34
  505.1 5.5 fusion.43
  510.6 0.8 compare_select_fusion.4
  511.4 0.8 gather_fusion.1
  512.2 1.2 convolution_add_fusion.2
  513.6 1.3 copy.45
  515.0 15.2 %fusion.11 = f32[256,256]{0,1:T(8,128)S(1)} fusion(bf16[32768,256]{0,1:T(8,128)(2,1)} %all-gather.5.cloned.1.call-done, f32[256,256]{0,1:T(8,128)} %all-reduce.3.cloned.1.call-done), kind=kOutput, calls=%fused_computation.25 | convolution fusion | flops 4295163904 | bytes 17301504 | tf_op jit(solution)/shard_map/dot_general | solution.py:28
  530.4 11.7 %cholesky.50 = f32[128,128]{1,0:T(8,128)S(1)} custom-call(f32[128,128]{1,0:T(8,128)S(1)} %cholesky.118), custom_call_target="Cholesky" | custom-call | tf_op jit(solution)/shard_map/jit(cholesky)/cholesky | solution.py:94
  542.1 9.8 %custom-call.18 = f32[1,128,128]{1,2,0:T(8,128)S(1)} custom-call(f32[1,128,128]{2,1,0:T(8,128)S(1)} %get-tuple-element.439), custom_call_target="InvertDiagBlocksLowerTriangular" | custom-call | tf_op jit(solution)/shard_map/jit(cholesky)/cholesky | solution.py:94
  552.5 11.9 %cholesky.105 = f32[128,128]{1,0:T(8,128)S(1)} custom-call(f32[128,128]{1,0:T(8,128)S(1)} %convolution_subtract_fusion.2), custom_call_target="Cholesky" | custom-call | tf_op jit(solution)/shard_map/jit(cholesky)/cholesky | solution.py:94
  564.4 0.7 compare_reduce_fusion
  566.5 4.1 while.17
  566.5 0.7 fusion.40
  567.2 1.3 bitcast_dynamic-update-slice_fusion.2
  568.6 0.7 fusion.40
  569.2 1.3 bitcast_dynamic-update-slice_fusion.2
  570.6 19.7 %custom-call.19 = f32[2,128,128]{1,2,0:T(8,128)S(1)} custom-call(f32[2,128,128]{2,1,0:T(8,128)S(1)} %get-tuple-element.332), custom_call_target="InvertDiagBlocksLowerTriangular" | custom-call | tf_op jit(solution)/shard_map/jit(_cho_solve)/triangular_solve | solution.py:95
  590.3 1.1 fusion.13
  591.4 1.0 convolution_subtract_fusion.1
  593.0 0.3 convolution_subtract_fusion
  593.5 10.3 %all_to_all.31 = f32[128,16,16]{0,2,1:T(8,128)S(1)} all-to-all(f32[128,16,16]{0,2,1:T(8,128)S(1)} %bitcast.75), channel_id=1, replica_groups=mesh['rows'=16,'cols'=8] {'rows'}, dimensions={1} | all-to-all | bytes 262144 | tf_op jit(solution)/shard_map/all_to_all | solution.py:97
  604.0 8.1 %all_to_all.32 = f32[8,256,16]{1,2,0:T(8,128)S(1)} all-to-all(f32[8,256,16]{1,2,0:T(8,128)S(1)} %copy.47), channel_id=1, replica_groups=mesh['rows'=16,'cols'=8] {'cols'}, dimensions={0} | all-to-all | bytes 262144 | tf_op jit(solution)/shard_map/all_to_all | solution.py:96
  612.3 0.7 copy.54
  (45 shorter events, 2.4 us)
Async XLA Ops:
  6.5 52.8 %all-gather.3.cloned.1.call-start = ((), (), s32[]{:S(2)}) async-start(), calls=%async_computation.4 | async-start | bytes 1114112 | tf_op jit(solution)/shard_map/all_gather | solution.py:58
  7.3 162.9 %all-gather.5.cloned.1.call-start = ((), (), s32[]{:S(2)}) async-start(), calls=%async_computation.6 | async-start | bytes 17825792 | tf_op jit(solution)/shard_map/all_gather | solution.py:60
  27.3 487.7 %all-reduce.3.cloned.1.call-start = ((), (), s32[]{:S(2)}) async-start(), calls=%async_computation.5 | async-start | bytes 524288 | tf_op jit(solution)/shard_map/psum | solution.py:63
  62.1 528.2 %reduce-scatter.2.cloned.1.call-start = ((), (), s32[]{:S(2)}) async-start(), calls=%async_computation.7 | async-start | bytes 1179648 | tf_op jit(solution)/shard_map/reduce_scatter | solution.py:93
Sparse Core Ops, SparseCore 0:
  9.8 49.4 all-gather.2
  61.7 108.4 all-gather.4
  172.7 64.6 all-reduce.2
  515.1 30.7 reduce-scatter.1
where the time goes:
time: 625 us; the launch traced here: 619 us
  local copies, waits for them, and re-layouts  317 us (51%)
  waiting for transfers between devices  139 us (22%)
  other arithmetic  85.4 us (14%)
  blocking collectives  36.3 us (6%)
  matrix products  26.3 us (4%)
  between operations  14.6 us (2%)
    gather x4, local copies, waits for them, and re-layouts, block_fold(): picked = table[third.reshape(group * width)]  275 us
    all_gather x1, waiting for transfers between devices, per_device(): third_whole = lax.all_gather(third_part, 'rows', axis=1, tiled=True)  107 us
    another operation x6, other arithmetic, per_device(): factor = jnp.linalg.cholesky(gram)  34.2 us
    all_gather x1, waiting for transfers between devices, per_device(): second_range = lax.all_gather(second_factor, 'rows', axis=1, tiled=True)  31.9 us
    unnamed x3, local copies, waits for them, and re-layouts  24.6 us
    reduce_sum x4, other arithmetic, block_fold(): return jnp.sum(scaled.reshape(group, width, picked.shape[1]), axis=1)  21.8 us
    another operation x4, other arithmetic, per_device(): solved = jax.scipy.linalg.cho_solve((factor, True), mine.T).T  19.7 us
    dot_general x2, matrix products, gram_product(): lax.dot_general(left, right, contract, preferred_element_type=jnp.float32)  18 us
  transfers between devices with their start and end apart: 4, of which 2 were waited for; matrix products, arithmetic and copies ran while one was open for 69% of the time, Pallas kernels for 0%

commit v1 on v0

v1 whole, which is shorter than its diff:
```python
import jax
import jax.numpy as jnp
from jax import lax
from jax.experimental import pallas as pl
from jax.experimental.pallas import tpu as pltpu
from jax.sharding import PartitionSpec as P

F32 = jnp.float32
BF = jnp.bfloat16
MESH = pl.DeviceIdType.MESH
NT = (((1,), (1,)), ((), ()))
NN = (((1,), (0,)), ((), ()))
HIGH = lax.Precision.HIGHEST
VMEM = pltpu.VMEM
ANY = pl.BlockSpec(memory_space=pl.ANY)
INV = pl.BlockSpec(memory_space=pltpu.VMEM)

PARTS = ((0, 1408), (1408, 1408), (2816, 1280))
ORDERS = ("xyz", "yzx", "zxy")
SEMS = 28 * 3 + 16 * 3


def place():
    r, c = lax.axis_index("rows"), lax.axis_index("cols")
    return {"z": lax.div(r, 8) * 2 + lax.rem(c, 2), "x": lax.rem(lax.div(r, 2), 4), "k": lax.rem(r, 2), "y": lax.div(c, 2)}


def device(at):
    return (lax.div(at["z"], 2) * 8 + at["x"] * 2 + at["k"], at["y"] * 2 + lax.rem(at["z"], 2))


def moved(at, dim, step):
    return {**at, dim: lax.rem(at[dim] + step, 4)}


class Gather:
    def __init__(self, t, send, recv):
        self.t, self.send, self.recv = t, send, recv
        self.me = place()
        self.used = 0
        self.sent = []

    def block(self, part, at, half=None):
        start, size = PARTS[part]
        if half is not None:
            first = (size // 128 // 2) * 128
            start, size = (start, first) if half == 0 else (start + first, size - first)
        return self.t.at[at["z"], at["x"], at["k"], at["y"], :, pl.ds(start, size)]

    def set_of(self, part, at, whole):
        start, size = PARTS[part]
        return self.t.at[*[slice(None) if d in whole else at[d] for d in "zxky"], :, pl.ds(start, size)]

    def new(self):
        self.used += 1
        return self.used - 1

    def copy(self, ref, n, to):
        c = pltpu.make_async_remote_copy(ref, ref, self.send.at[n], self.recv.at[n], device_id=device(to), device_id_type=MESH)
        c.start()
        self.sent.append(c)

    def arrived(self, ref, n):
        pltpu.make_async_remote_copy(ref, ref, self.send.at[n], self.recv.at[n], device_id=device(self.me), device_id_type=MESH).wait_recv()

    def run(self):
        me = self.me
        FORE, BACK = 1, 3
        parts = range(3)
        one = {(p, s): self.new() for p in parts for s in (FORE, BACK)}
        onef = {(p, s): self.new() for p in parts for s in (FORE, BACK)}
        two = {(p, o, s): self.new() for p in parts for o in range(4) for s in (FORE, BACK)}
        twof = {(p, o): self.new() for p in parts for o in range(4)}
        three = {(p, o, s): self.new() for p in parts for o in range(4) for s in (FORE, BACK)}
        threef = {(p, o): self.new() for p in parts for o in range(4)}
        core = {(p, a, b): self.new() for p in parts for a in range(4) for b in range(4)}
        other = {**me, "k": 1 - me["k"]}

        def dims(p):
            return ORDERS[p]

        def at1(p, a):
            return moved(me, dims(p)[0], a)

        def at2(p, a, b):
            return moved(at1(p, a), dims(p)[1], b)

        def set3(p, b, c, k=None):
            d = dims(p)
            at = moved(moved(me, d[1], b), d[2], c)
            if k is not None:
                at = {**at, "k": k}
            return self.set_of(p, at, d[0])

        def to(p, i, s):
            return moved(me, dims(p)[i], s)

        def cross(p, b, c):
            self.copy(set3(p, b, c), core[p, b, c], other)

        for p in parts:
            for s in (FORE, BACK):
                self.copy(self.block(p, me), one[p, s], to(p, 0, s))
        for p in parts:
            for s in (FORE, BACK):
                self.copy(self.block(p, me), two[p, 0, s], to(p, 1, s))
        for p in parts:
            for s in (FORE, BACK):
                back = 4 - s
                self.arrived(self.block(p, at1(p, back)), one[p, s])
                self.copy(self.block(p, at1(p, back), half=0 if s == FORE else 1), onef[p, s], to(p, 0, s))
                for s2 in (FORE, BACK):
                    self.copy(self.block(p, at1(p, back)), two[p, back, s2], to(p, 1, s2))
        for p in parts:
            for s in (FORE, BACK):
                self.arrived(self.block(p, at1(p, 2), half=0 if s == FORE else 1), onef[p, s])
            for s2 in (FORE, BACK):
                self.copy(self.block(p, at1(p, 2)), two[p, 2, s2], to(p, 1, s2))
            for s3 in (FORE, BACK):
                self.copy(set3(p, 0, 0), three[p, 0, s3], to(p, 2, s3))
            cross(p, 0, 0)
        FIRST = {FORE: (0, 3), BACK: (1, 2)}
        for p in parts:
            for o in (0, 3, 1, 2):
                for s in (FORE, BACK):
                    back = 4 - s
                    self.arrived(self.block(p, at2(p, o, back)), two[p, o, s])
                    if o in FIRST[s]:
                        self.copy(self.block(p, at2(p, o, back)), twof[p, o], to(p, 1, s))
        for p in parts:
            for b in (3, 1):
                for s3 in (FORE, BACK):
                    self.copy(set3(p, b, 0), three[p, b, s3], to(p, 2, s3))
                cross(p, b, 0)
        for p in parts:
            for o in (0, 3, 1, 2):
                self.arrived(self.block(p, at2(p, o, 2)), twof[p, o])
            for s3 in (FORE, BACK):
                self.copy(set3(p, 2, 0), three[p, 2, s3], to(p, 2, s3))
            cross(p, 2, 0)
        yield
        for b in (0, 3, 1, 2):
            for p in parts:
                for s in (FORE, BACK):
                    back = 4 - s
                    self.arrived(set3(p, b, back), three[p, b, s])
                    if b in FIRST[s]:
                        self.copy(set3(p, b, back), threef[p, b], to(p, 2, s))
                    cross(p, b, back)
        yield
        for b in (0, 3, 1, 2):
            for p in parts:
                self.arrived(set3(p, b, 2), threef[p, b])
                cross(p, b, 2)
        for p in parts:
            for a in range(4):
                for b in range(4):
                    self.arrived(set3(p, a, b, k=1 - me["k"]), core[p, a, b])
        for c in self.sent:
            c.wait_send()


def send_to(src, dst, ssem, rsem, to):
    c = pltpu.make_async_remote_copy(src, dst, ssem, rsem, device_id=to, device_id_type=MESH)
    c.start()
    return c


def k1_body(piece, spiece, t, s_out, gs_out, s_vm, part, parts, mine, send, recv, ssem, srecv, csem, crecv, gsem, grecv, lsem):
    g = Gather(t, send, recv)
    me = g.me
    r, c = lax.axis_index("rows"), lax.axis_index("cols")
    cp = pltpu.make_async_copy(piece, t.at[me["z"], me["x"], me["k"], me["y"]], lsem.at[0])
    cp.start()
    cs = pltpu.make_async_copy(spiece, s_vm.at[r], lsem.at[1])
    cs.start()
    sent = []
    for i in range(1, 16):
        to = lax.rem(r + i, 16)
        sent.append(send_to(spiece, s_vm.at[r], ssem.at[i - 1], srecv.at[i - 1], (to, c)))
    cp.wait()
    cs.wait()
    run = g.run()
    next(run)
    for i in range(1, 16):
        got = s_vm.at[lax.rem(r + 16 - i, 16)]
        pltpu.make_async_remote_copy(got, got, ssem.at[i - 1], srecv.at[i - 1], device_id=(r, c), device_id_type=MESH).wait_recv()
    whole = s_vm[...].reshape(256, 2048)
    chunk = lax.dot_general(s_vm[r], whole, NT, preferred_element_type=F32)
    part[...] = chunk
    parts[c] = chunk
    for i in range(1, 8):
        sent.append(send_to(part, parts.at[c], csem.at[i - 1], crecv.at[i - 1], (r, lax.rem(c + i, 8))))
    out = pltpu.make_async_copy(s_vm, s_out, lsem.at[2])
    out.start()
    next(run)
    for i in range(1, 8):
        got = parts.at[lax.rem(c + 8 - i, 8)]
        pltpu.make_async_remote_copy(got, got, csem.at[i - 1], crecv.at[i - 1], device_id=(r, c), device_id_type=MESH).wait_recv()
    mine[...] = sum(parts[i] for i in range(8))
    keep = pltpu.make_async_copy(mine, gs_out.at[r], lsem.at[3])
    keep.start()
    for i in range(1, 16):
        sent.append(send_to(mine, gs_out.at[r], gsem.at[i - 1], grecv.at[i - 1], (lax.rem(r + i, 16), c)))
    for _ in run:
        pass
    for i in range(1, 16):
        got = gs_out.at[lax.rem(r + 16 - i, 16)]
        pltpu.make_async_remote_copy(got, got, gsem.at[i - 1], grecv.at[i - 1], device_id=(r, c), device_id_type=MESH).wait_recv()
    out.wait()
    keep.wait()
    for x in sent:
        x.wait_send()


def k1(piece, spiece):
    D = pltpu.SemaphoreType.DMA
    return pl.pallas_call(
        k1_body,
        out_shape=(
            jax.ShapeDtypeStruct((4, 4, 2, 4, 16, 4096), BF),
            jax.ShapeDtypeStruct((16, 16, 2048), BF),
            jax.ShapeDtypeStruct((16, 16, 256), F32),
        ),
        in_specs=[ANY, ANY],
        out_specs=(ANY, ANY, ANY),
        scratch_shapes=[
            VMEM((16, 16, 2048), BF), VMEM((16, 256), F32), VMEM((8, 16, 256), F32), VMEM((16, 256), F32),
            D((SEMS,)), D((SEMS,)), D((15,)), D((15,)), D((7,)), D((7,)), D((15,)), D((15,)), D((4,)),
        ],
        compiler_params=pltpu.CompilerParams(has_side_effects=True),
        name="gather_factors",
    )(piece, spiece)

UB = 16
PAD = 136


def spread_step(step, base, q_ref, p_ref, v_ref, wf, whi, wlo):
    iq = lax.broadcasted_iota(jnp.int32, (128, 128), 0).astype(F32).astype(BF)
    ip = lax.broadcasted_iota(jnp.int32, (256, 128), 0).astype(F32).astype(BF)
    zero = jnp.zeros((128, 128), BF)
    one = jnp.ones((), BF)

    def row(ref, b, n):
        r = jnp.broadcast_to(ref[pl.ds(b, 1), :], (16, 128)).astype(BF)
        return jnp.concatenate([r] * (n // 16), axis=0)

    for pair in range(UB // 2):
        qs, ps = [], []
        for j in range(2):
            b = base + step * UB + 2 * pair + j
            qm = iq == row(q_ref, b, 128)
            qs.append(jnp.where(qm, row(v_ref, b, 128), zero))
            ps.append(jnp.where(ip == row(p_ref, b, 256), one, jnp.zeros((), BF)))
        lhs = jnp.concatenate([jnp.concatenate([qs[0], zero], 1), jnp.concatenate([zero, qs[1]], 1)], 0)
        rhs = jnp.concatenate(ps, 1)
        w = lax.dot_general(lhs, rhs, NT, preferred_element_type=F32)
        for j in range(2):
            for h in range(2):
                wf[h, pl.ds((2 * pair + j) * PAD, 128), :] = w[j * 128:(j + 1) * 128, h * 128:(h + 1) * 128]

    rows = pl.ds(pl.multiple_of(step * UB, UB), UB)

    def split(q8, _):
        for i in range(8):
            q = q8 * 8 + i
            for h in range(2):
                f = wf[h, pl.ds(q, UB, stride=PAD), :]
                hi = f.astype(BF)
                lo = (f - hi.astype(F32)).astype(BF)
                lanes = pl.ds(pl.multiple_of(q * 256, 256) + h * 128, 128)
                whi[rows, lanes] = hi
                wlo[rows, lanes] = lo
        return 0

    lax.fori_loop(0, 16, split, 0)


GRP = 256
KC = 2048


def k2_body(q_ref, p_ref, v_ref, sec_ref, own_ref, t_hbm, s_ref, out_ref, gt_ref, wf, whi, wlo, tbuf, fold, tsem):
    cps = []
    for c in range(8):
        for z in range(2):
            cps.append(pltpu.make_async_copy(t_hbm.at[z * 2 + c % 2, :, :, c // 2], tbuf.at[c, z], tsem.at[c * 2 + z]))
            cps[-1].start()
    gt_ref[...] = jnp.zeros((256, 256), F32)
    for g in range(512 // GRP):
        def st(i, _):
            spread_step(i, g * GRP, q_ref, p_ref, v_ref, wf, whi, wlo)
            return 0
        lax.fori_loop(0, GRP // UB, st, 0)
        if g == 0:
            for c in cps:
                c.wait()
        grow = pl.ds(g * GRP, GRP)
        fold[grow, :] = jnp.zeros((GRP, 256), F32)

        def mm(i, _):
            c = lax.div(i, 4096 // KC)
            k0 = pl.multiple_of(lax.rem(i, 4096 // KC) * KC, KC)
            t = tbuf[c, :, :, :, :, pl.ds(k0, KC)].reshape(256, KC)
            ks = pl.ds(pl.multiple_of(i * KC, KC), KC)
            lhs = jnp.concatenate([whi[:, ks], wlo[:, ks]] + ([t] if g == 0 else []), 0)
            r = lax.dot_general(lhs, t, NT, preferred_element_type=F32)
            fold[grow, :] += r[:GRP] + r[GRP:2 * GRP]
            if g == 0:
                gt_ref[...] += r[2 * GRP:]
            return 0
        lax.fori_loop(0, 32768 // KC, mm, 0)
    one, zero = jnp.ones((), BF), jnp.zeros((), BF)
    ij = lax.broadcasted_iota(jnp.int32, (2048, 512), 0)
    pick = jnp.where(ij == sec_ref[...], one, zero)
    second = lax.dot_general(s_ref[...].reshape(256, 2048), pick, NN, preferred_element_type=F32)
    contrib = second * fold[...].T
    hi = contrib.astype(BF)
    rest = contrib - hi.astype(F32)
    mid = rest.astype(BF)
    low = (rest - mid.astype(F32)).astype(BF)
    ii = lax.broadcasted_iota(jnp.int32, (1024, 512), 0)
    put = jnp.where(ii == own_ref[...], one, zero)
    r = lax.dot_general(jnp.concatenate([hi, mid, low], 0), put, NT, preferred_element_type=F32)
    total = r[:256] + (r[256:512] + r[512:])
    for c in range(8):
        out_ref[c] = total[:, c * 128:(c + 1) * 128]


def k2(q, p, v, sec, own, t, s):
    return pl.pallas_call(
        k2_body,
        out_shape=(jax.ShapeDtypeStruct((8, 256, 128), F32), jax.ShapeDtypeStruct((256, 256), F32)),
        in_specs=[INV] * 5 + [ANY, INV],
        out_specs=(INV, INV),
        scratch_shapes=[
            VMEM((2, UB * PAD, 128), F32),
            VMEM((GRP, 32768), BF),
            VMEM((GRP, 32768), BF),
            VMEM((8, 2, 4, 2, 16, 4096), BF),
            VMEM((512, 256), F32),
            pltpu.SemaphoreType.DMA((16,)),
        ],
        compiler_params=pltpu.CompilerParams(vmem_limit_bytes=67043328),
        name="spread_fold",
    )(q, p, v, sec, own, t, s)


def inverse_body(gs_ref, gt_ref, out_ref, a_ref, x_ref):
    gram = (gs_ref[...].reshape(256, 256) / 16384) * (gt_ref[...] / 32768)
    eye = (lax.broadcasted_iota(jnp.int32, (256, 256), 0) == lax.broadcasted_iota(jnp.int32, (256, 256), 1)).astype(F32)
    diag = gram * eye
    down = 1 / jnp.sqrt(jnp.sum(diag, axis=1, keepdims=True))
    along = 1 / jnp.sqrt(jnp.sum(diag, axis=0, keepdims=True))
    a = gram * down * along
    a_ref[...] = a
    bound = jnp.max(jnp.sum(jnp.abs(a), axis=0))
    x_ref[...] = eye * (2 / (1 + bound))

    def dot(u, w):
        return lax.dot_general(u, w, NN, precision=HIGH, preferred_element_type=F32)

    def go(state):
        return (state[0] < 64) & (state[1] > 1e-4)

    def step(state):
        x = x_ref[...]
        rest = eye - dot(a_ref[...], x)
        x_ref[...] = x + dot(x, rest)
        return state[0] + 1, jnp.max(jnp.abs(rest))

    lax.while_loop(go, step, (0, jnp.float32(1.0)))
    out_ref[...] = x_ref[...] * down * along


def inverse(gs, gt):
    return pl.pallas_call(
        inverse_body,
        out_shape=jax.ShapeDtypeStruct((256, 256), F32),
        in_specs=[INV, INV],
        out_specs=INV,
        scratch_shapes=[VMEM((256, 256), F32), VMEM((256, 256), F32)],
        name="gram_inverse",
    )(gs, gt)


def k3_body(part, inv, out, got, x, rsem, rrecv, xsem, xrecv, lsem):
    r, c = lax.axis_index("rows"), lax.axis_index("cols")
    sent = []
    for i in range(1, 8):
        to = lax.rem(c + i, 8)
        sent.append(send_to(part.at[to], got.at[i - 1], rsem.at[i - 1], rrecv.at[i - 1], (r, to)))
    total = part[c]
    for i in range(7):
        pltpu.make_async_remote_copy(got.at[i], got.at[i], rsem.at[i], rrecv.at[i], device_id=(r, c), device_id_type=MESH).wait_recv()
        total = total + got[i]
    solved = lax.dot_general(inv[...], total, NN, precision=HIGH, preferred_element_type=F32)
    x[...] = solved.reshape(16, 16, 128)
    home = lax.div(r, 2)
    slot = lax.rem(r, 2) * 8 + c
    mine = home == c
    lanes = pl.ds(pl.multiple_of(slot * 128, 128), 128)
    for i in range(1, 16):
        to = lax.rem(r + i, 16)
        sent.append(send_to(x.at[to], out.at[:, lanes], xsem.at[i], xrecv.at[slot], (to, home)))

    near = pltpu.make_async_copy(x.at[r], out.at[:, lanes], lsem)
    far = pltpu.make_async_remote_copy(x.at[r], out.at[:, lanes], xsem.at[0], xrecv.at[slot], device_id=(r, home), device_id_type=MESH)

    @pl.when(mine)
    def _():
        near.start()

    @pl.when(jnp.logical_not(mine))
    def _():
        far.start()

    for i in range(16):
        there = out.at[:, pl.ds(i * 128, 128)]
        take = pltpu.make_async_remote_copy(there, there, xsem.at[0], xrecv.at[i], device_id=(r, c), device_id_type=MESH)

        @pl.when(jnp.logical_not(mine & (slot == i)))
        def _():
            take.wait_recv()

    @pl.when(mine)
    def _():
        near.wait()

    @pl.when(jnp.logical_not(mine))
    def _():
        far.wait_send()

    for s in sent:
        s.wait_send()


def k3(part, inv):
    D = pltpu.SemaphoreType.DMA
    return pl.pallas_call(
        k3_body,
        out_shape=jax.ShapeDtypeStruct((16, 2048), F32),
        in_specs=[INV, INV],
        out_specs=INV,
        scratch_shapes=[VMEM((7, 256, 128), F32), VMEM((16, 16, 128), F32), D((7,)), D((7,)), D((16,)), D((16,)), D(())],
        compiler_params=pltpu.CompilerParams(has_side_effects=True),
        name="reduce_solve_place",
    )(part, inv)


def per_device(values, length, owner, second, third, live_blocks, second_factor, third_factor):
    r, c = lax.axis_index("rows"), lax.axis_index("cols")
    lane = jnp.arange(128, dtype=jnp.int32)
    slot = jnp.arange(512, dtype=jnp.int32)
    live = (lane[None, :] < length[:, None]) & (slot < live_blocks[0])[:, None]
    v = jnp.where(live, values, jnp.zeros((), BF)).astype(F32)
    q = (third >> 8).astype(F32)
    p = (third & 255).astype(F32)
    sec = (second - c * 2048).reshape(1, 512)
    own = (owner - r * 1024).reshape(1, 512)
    t, s, gs = k1(third_factor.T, second_factor.T)
    part, gt = k2(q, p, v, sec, own, t, s)
    inv = inverse(gs, gt)
    return k3(part, inv).T


def solution(mesh):
    both = P(("rows", "cols"))
    wide = P(("rows", "cols"), None)
    return jax.shard_map(
        per_device,
        mesh=mesh,
        in_specs=(wide, both, both, both, wide, both, P("cols", "rows"), P("cols", "rows")),
        out_specs=P("cols", "rows"),
        check_vma=False,
    )
```

time: 625 us -> 192 us (0.31)
  local copies, waits for them, and re-layouts: 317 us -> 1.57 us
  Pallas kernels: 0 us -> 183 us
  waiting for transfers between devices: 139 us -> 0 us
  other arithmetic: 85.4 us -> 6.15 us
  blocking collectives: 36.3 us -> 0 us
  matrix products: 26.3 us -> 0 us
  between operations: 14.6 us -> 0.69 us
    gather x8 -> x0, local copies, waits for them, and re-layouts: 278 us -> none  [the longest x4 275 us: block_fold(): picked = table[third.reshape(group * width)]]
    pallas_call x0 -> x4, Pallas kernels: none -> 183 us  [the longest x1 69.9 us: k2(): pl.pallas_call(k2_body, out_shape=(jax.ShapeDtypeStruct((8, 256, 128), F3...]
    all_gather x2 -> x0, waiting for transfers between devices: 138 us -> none  [the longest x1 107 us: per_device(): third_whole = lax.all_gather(third_part, 'rows', axis=1, tiled=True)]
    another operation x10 -> x0, other arithmetic: 54 us -> none  [the longest x6 34.2 us: per_device(): factor = jnp.linalg.cholesky(gram)]
    all_to_all x3 -> x0, blocking collectives: 36.3 us -> none  [the longest x1 17.8 us: from_everyone(): lax.all_to_all(jnp.broadcast_to(value[None], (size, *value.shape)), axis,...]
    unnamed x3 -> x1, local copies, waits for them, and re-layouts: 24.6 us -> 1.57 us
    dot_general x6 -> x0, matrix products: 22.7 us -> none  [the longest x2 18 us: gram_product(): lax.dot_general(left, right, contract, preferred_element_type=jnp.float32)]
    reduce_sum x4 -> x0, other arithmetic: 21.8 us -> none  [block_fold(): return jnp.sum(scaled.reshape(group, width, picked.shape[1]), axis=1)]
  transfers between devices with their start and end apart: 4 -> 0, of which waited for: 2 -> 0; matrix products, arithmetic and copies ran while one was open for 69% -> 0% of each run, Pallas kernels for 0% -> 0%
where the time goes in v1:
time: 192 us; the launch traced here: 191 us
  Pallas kernels  183 us (95%)
  other arithmetic  6.15 us (3%)
    pallas_call x1, Pallas kernels, k2(): pl.pallas_call(k2_body, out_shape=(jax.ShapeDtypeStruct((8, 256, 128), F3...  69.9 us
    pallas_call x1, Pallas kernels, k1(): pl.pallas_call(k1_body, out_shape=(jax.ShapeDtypeStruct((4, 4, 2, 4, 16,...  69.7 us
    pallas_call x1, Pallas kernels, k3(): pl.pallas_call(k3_body, out_shape=jax.ShapeDtypeStruct((16, 2048), F32),...  33.6 us
    pallas_call x1, Pallas kernels, inverse(): pl.pallas_call(inverse_body, out_shape=jax.ShapeDtypeStruct((256, 256), F...  9.78 us

profile of v1, /device:TPU:25, one launch (start us, length us, event | category | flops | bytes accessed | tf_op | source)
XLA Modules:
  0.0 191.3 jit_solution(6063207227596233178)
XLA Ops:
  0.7 1.3 broadcast_subtract_fusion
  1.9 1.3 broadcast_subtract_fusion.1
  3.2 1.8 fusion.2.v_ref
  5.0 1.8 and_convert_fusion
  6.8 69.7 %gather_factors.1 = (bf16[4,4,2,4,16,4096]{5,4,3,2,1,0:T(8,128)(2,1)}, bf16[16,16,2048]{2,1,0:T(8,128)(2,1)}, f32[16,16,256]{2,1,0:T(8,128)}) custom-call(bf16[16,4096]{1,0:T(8,128)(2,1)} %bitcast.8, bf16[16,2048]{1,0:T(8,128)(2,1)} %bitcast.9), custom_call_target="tpu_custom_call" | custom-call | tf_op jit(solution)/shard_map/gather_factors/pallas_call | solution.py:218
  76.5 69.9 %spread_fold.1 = (f32[8,256,128]{2,1,0:T(8,128)}, f32[256,256]{1,0:T(8,128)}) custom-call(f32[512,128]{1,0:T(8,128)} %get-tuple-element.16.q_ref, f32[512,128]{1,0:T(8,128)} %get-tuple-element.15.p_ref, f32[512,128]{1,0:T(8,128)} %fusion.2.v_ref, s32[1,512]{1,0:T(1,128)} %bitcast.11, s32[1,512]{1,0:T(1,128)} %bitcast.10, ...), custom_call_target="tpu_custom_call" | custom-call | tf_op jit(solution)/shard_map/spread_fold/pallas_call | solution.py:332
  146.4 9.8 %gram_inverse.1.inv = f32[256,256]{1,0:T(8,128)} custom-call(f32[16,16,256]{2,1,0:T(8,128)} %get-tuple-element.13.gs_ref, f32[256,256]{1,0:T(8,128)} %get-tuple-element.14.gt_ref), custom_call_target="tpu_custom_call" | custom-call | tf_op jit(solution)/shard_map/gram_inverse/pallas_call | solution.py:378
  156.2 33.6 %reduce_solve_place.1 = f32[16,2048]{1,0:T(8,128)} custom-call(f32[8,256,128]{2,1,0:T(8,128)} %get-tuple-element.12.part, f32[256,256]{1,0:T(8,128)} %gram_inverse.1.inv), custom_call_target="tpu_custom_call" | custom-call | tf_op jit(solution)/shard_map/reduce_solve_place/pallas_call | solution.py:441
  189.7 1.6 copy.11
  (1 shorter events, 0.0 us)

commit v2 on v1

v2 whole, which is shorter than its diff:
```python
import jax
import jax.numpy as jnp
from jax import lax
from jax.experimental import pallas as pl
from jax.experimental.pallas import tpu as pltpu
from jax.sharding import PartitionSpec as P

F32 = jnp.float32
BF = jnp.bfloat16
MESH = pl.DeviceIdType.MESH
NT = (((1,), (1,)), ((), ()))
NN = (((1,), (0,)), ((), ()))
HIGH = lax.Precision.HIGHEST
VMEM = pltpu.VMEM
ANY = pl.BlockSpec(memory_space=pl.ANY)
INV = pl.BlockSpec(memory_space=pltpu.VMEM)

PARTS = ((0, 1408), (1408, 1408), (2816, 1280))
ORDERS = ("xyz", "yzx", "zxy")
SEMS = 28 * 3 + 16 * 3


def place():
    r, c = lax.axis_index("rows"), lax.axis_index("cols")
    return {"z": lax.div(r, 8) * 2 + lax.rem(c, 2), "x": lax.rem(lax.div(r, 2), 4), "k": lax.rem(r, 2), "y": lax.div(c, 2)}


def device(at):
    return (lax.div(at["z"], 2) * 8 + at["x"] * 2 + at["k"], at["y"] * 2 + lax.rem(at["z"], 2))


class Gather:
    def __init__(self, t, send, recv):
        self.t, self.send, self.recv = t, send, recv
        self.me = me = place()
        self.mine = device(me)
        self.steps = {d: [me[d], *(lax.rem(me[d] + i, 4) for i in (1, 2, 3))] for d in "zxy"}
        self.other = {**me, "k": 1 - me["k"]}
        self.used = 0
        self.sent = []

    def moved(self, at, dim, step):
        return {**at, dim: self.steps[dim][step]}

    def block(self, part, at, half=None):
        start, size = PARTS[part]
        if half is not None:
            first = (size // 128 // 2) * 128
            start, size = (start, first) if half == 0 else (start + first, size - first)
        return self.t.at[at["z"], at["x"], at["k"], at["y"], :, pl.ds(start, size)]

    def set_of(self, part, at, whole):
        start, size = PARTS[part]
        return self.t.at[*[slice(None) if d in whole else at[d] for d in "zxky"], :, pl.ds(start, size)]

    def new(self):
        self.used += 1
        return self.used - 1

    def copy(self, ref, n, to):
        c = pltpu.make_async_remote_copy(ref, ref, self.send.at[n], self.recv.at[n], device_id=device(to), device_id_type=MESH)
        c.start()
        self.sent.append((ref, n))

    def arrived(self, ref, n):
        pltpu.make_async_remote_copy(ref, ref, self.send.at[n], self.recv.at[n], device_id=self.mine, device_id_type=MESH).wait_recv()

    def run(self):
        me = self.me
        FORE, BACK = 1, 3
        parts = range(3)
        one = {(p, s): self.new() for p in parts for s in (FORE, BACK)}
        onef = {(p, s): self.new() for p in parts for s in (FORE, BACK)}
        two = {(p, o, s): self.new() for p in parts for o in range(4) for s in (FORE, BACK)}
        twof = {(p, o): self.new() for p in parts for o in range(4)}
        three = {(p, o, s): self.new() for p in parts for o in range(4) for s in (FORE, BACK)}
        threef = {(p, o): self.new() for p in parts for o in range(4)}
        core = {(p, a, b): self.new() for p in parts for a in range(4) for b in range(4)}

        def dims(p):
            return ORDERS[p]

        def at1(p, a):
            return self.moved(me, dims(p)[0], a)

        def at2(p, a, b):
            return self.moved(at1(p, a), dims(p)[1], b)

        def set3(p, b, c, k=None):
            d = dims(p)
            at = self.moved(self.moved(me, d[1], b), d[2], c)
            if k is not None:
                at = {**at, "k": k}
            return self.set_of(p, at, d[0])

        def to(p, i, s):
            return self.moved(me, dims(p)[i], s)

        def cross(p, b, c):
            self.copy(set3(p, b, c), core[p, b, c], self.other)

        for p in parts:
            for s in (FORE, BACK):
                self.copy(self.block(p, me), one[p, s], to(p, 0, s))
        for p in parts:
            for s in (FORE, BACK):
                self.copy(self.block(p, me), two[p, 0, s], to(p, 1, s))
        yield
        for p in parts:
            for s in (FORE, BACK):
                back = 4 - s
                self.arrived(self.block(p, at1(p, back)), one[p, s])
                self.copy(self.block(p, at1(p, back), half=0 if s == FORE else 1), onef[p, s], to(p, 0, s))
                for s2 in (FORE, BACK):
                    self.copy(self.block(p, at1(p, back)), two[p, back, s2], to(p, 1, s2))
        yield
        for p in parts:
            for s in (FORE, BACK):
                self.arrived(self.block(p, at1(p, 2), half=0 if s == FORE else 1), onef[p, s])
            for s2 in (FORE, BACK):
                self.copy(self.block(p, at1(p, 2)), two[p, 2, s2], to(p, 1, s2))
            for s3 in (FORE, BACK):
                self.copy(set3(p, 0, 0), three[p, 0, s3], to(p, 2, s3))
            cross(p, 0, 0)
        yield
        FIRST = {FORE: (0, 3), BACK: (1, 2)}
        for p in parts:
            for o in (0, 3, 1, 2):
                for s in (FORE, BACK):
                    back = 4 - s
                    self.arrived(self.block(p, at2(p, o, back)), two[p, o, s])
                    if o in FIRST[s]:
                        self.copy(self.block(p, at2(p, o, back)), twof[p, o], to(p, 1, s))
            for b in (3, 1):
                for s3 in (FORE, BACK):
                    self.copy(set3(p, b, 0), three[p, b, s3], to(p, 2, s3))
                cross(p, b, 0)
        yield
        for p in parts:
            for o in (0, 3, 1, 2):
                self.arrived(self.block(p, at2(p, o, 2)), twof[p, o])
            for s3 in (FORE, BACK):
                self.copy(set3(p, 2, 0), three[p, 2, s3], to(p, 2, s3))
            cross(p, 2, 0)
        for b in (0, 3, 1, 2):
            yield
            for p in parts:
                for s in (FORE, BACK):
                    back = 4 - s
                    self.arrived(set3(p, b, back), three[p, b, s])
                    if b in FIRST[s]:
                        self.copy(set3(p, b, back), threef[p, b], to(p, 2, s))
                    cross(p, b, back)
        yield
        for b in (0, 3, 1, 2):
            for p in parts:
                self.arrived(set3(p, b, 2), threef[p, b])
                cross(p, b, 2)
        for p in parts:
            for a in range(4):
                for b in range(4):
                    self.arrived(set3(p, a, b, k=self.other["k"]), core[p, a, b])
        for ref, n in self.sent:
            pltpu.make_async_remote_copy(ref, ref, self.send.at[n], self.recv.at[n], device_id=self.mine, device_id_type=MESH).wait_send()


def send_to(src, dst, ssem, rsem, to):
    c = pltpu.make_async_remote_copy(src, dst, ssem, rsem, device_id=to, device_id_type=MESH)
    c.start()
    return c


UB = 16
STEPS = 512 // UB
GRP = 256
PAD = 129


def spread_pair(at, pair, q_ref, p_ref, v_ref, dst):
    iq = lax.broadcasted_iota(jnp.int32, (128, 128), 0).astype(F32).astype(BF)
    ip = lax.broadcasted_iota(jnp.int32, (256, 128), 0).astype(F32).astype(BF)
    zero = jnp.zeros((128, 128), BF)

    def row(ref, b, n):
        one = jnp.broadcast_to(ref[pl.ds(b, 1), :], (16, 128)).astype(BF)
        return jnp.concatenate([one] * (n // 16), axis=0)

    qs, ps = [], []
    for j in range(2):
        b = at + 2 * pair + j
        qs.append(jnp.where(iq == row(q_ref, b, 128), row(v_ref, b, 128), zero))
        ps.append(jnp.where(ip == row(p_ref, b, 256), jnp.ones((), BF), jnp.zeros((), BF)))
    lhs = jnp.concatenate([jnp.concatenate([qs[0], zero], 1), jnp.concatenate([zero, qs[1]], 1)], 0)
    w = lax.dot_general(lhs, jnp.concatenate(ps, 1), NT, preferred_element_type=F32)
    for j in range(2):
        for h in range(2):
            dst[h, pl.ds((2 * pair + j) * PAD, 128), :] = w[j * 128:(j + 1) * 128, h * 128:(h + 1) * 128]


def split_rows(q, rows, src, whi, wlo):
    for h in range(2):
        f = src[h, pl.ds(q, UB, stride=PAD), :]
        hi = f.astype(BF)
        whi[q * 2 + h, rows, :] = hi
        wlo[q * 2 + h, rows, :] = (f - hi.astype(F32)).astype(BF)


def spread_split(at, rows, q_ref, p_ref, v_ref, src, dst, whi, wlo):
    for pair in range(UB // 2):
        spread_pair(at, pair, q_ref, p_ref, v_ref, dst)
        for q in range(pair * 16, pair * 16 + 16):
            split_rows(q, rows, src, whi, wlo)


def send_to(src, dst, ssem, rsem, to):
    c = pltpu.make_async_remote_copy(src, dst, ssem, rsem, device_id=to, device_id_type=MESH)
    c.start()
    return c


def take(ref, sem, me):
    pltpu.make_async_remote_copy(ref, ref, sem, sem, device_id=me, device_id_type=MESH).wait_recv()


def main_body(piece, spiece, q_ref, p_ref, v_ref, sec_ref, own_ref, out_ref, gt_ref, gs_ref, spill,
              t, s_vm, part, parts, wfa, wfb, whi, wlo, fold,
              send, recv, ssem, srecv, csem, crecv, gsem, grecv, psem, lsem, lose):
    r, c = lax.axis_index("rows"), lax.axis_index("cols")
    g = Gather(t, send, recv)
    me = g.me
    cp = pltpu.make_async_copy(piece, t.at[me["z"], me["x"], me["k"], me["y"]], lsem.at[0])
    cp.start()
    cs = pltpu.make_async_copy(spiece, s_vm.at[r], lsem.at[1])
    cs.start()
    sent = []

    def push(src, dst, ssem, rsem, n, to):
        send_to(src, dst, ssem.at[n], rsem.at[n], to)
        sent.append((src, ssem, n))

    cp.wait()
    run = g.run()
    next(run)
    for i in range(1, 16):
        push(spiece, s_vm.at[r], ssem, srecv, i - 1, (lax.rem(r + i, 16), c))
    cs.wait()

    mine = gs_ref.at[r]

    def second_gram():
        for i in range(1, 16):
            take(s_vm.at[lax.rem(r + 16 - i, 16)], srecv.at[i - 1], (r, c))
        chunk = lax.dot_general(s_vm[r], s_vm[...].reshape(256, 2048), NT, preferred_element_type=F32)
        part[...] = chunk
        parts[c] = chunk
        for i in range(1, 8):
            push(part, parts.at[c], csem, crecv, i - 1, (r, lax.rem(c + i, 8)))

    def second_gram_sum():
        for i in range(1, 8):
            take(parts.at[lax.rem(c + 8 - i, 8)], crecv.at[i - 1], (r, c))
        gs_ref[r] = sum(parts[i] for i in range(8))
        for i in range(1, 16):
            push(mine, mine, gsem, grecv, i - 1, (lax.rem(r + i, 16), c))

    def park(step):
        rows = pl.ds(pl.multiple_of(step * UB, UB), UB)
        return (
            pltpu.make_async_copy(whi.at[:, rows, :], spill.at[0, :, rows, :], psem.at[0, step]),
            pltpu.make_async_copy(wlo.at[:, rows, :], spill.at[1, :, rows, :], psem.at[1, step]),
        )

    todo = {j: [] for j in range(STEPS // 2)}
    for j in EVENTS:
        todo[j].append(lambda: next(run))
    todo[GRAM_AT].append(second_gram)
    todo[SUM_AT].append(second_gram_sum)

    def iteration(i, _):
        for j in range(STEPS // 2):
            if todo[j]:
                @pl.when(i == j)
                def _():
                    for f in todo[j]:
                        f()
        for half in range(2):
            step = lax.rem(2 * i + half + STEPS - 1, STEPS)
            slot = lax.rem(step, 16)

            @pl.when((step >= 16) & (2 * i + half >= 1))
            def _():
                for x in park(slot):
                    x.wait()

            rows = pl.ds(pl.multiple_of(slot * UB, UB), UB)
            at = pl.multiple_of((2 * i + half) * UB, UB)
            src, dst = ((wfb, wfa), (wfa, wfb))[half]
            spread_split(at, rows, q_ref, p_ref, v_ref, src, dst, whi, wlo)

            @pl.when(step < 16)
            def _():
                for x in park(slot):
                    x.start()
        return 0

    lax.fori_loop(0, STEPS // 2, iteration, 0)
    for x in park(15):
        x.wait()
    for q in range(128):
        split_rows(q, pl.ds(GRP - UB, UB), wfb, whi, wlo)
    for _ in run:
        pass

    def back(i):
        tiles = pl.ds(pl.multiple_of(i * 32, 32), 32)
        return (
            pltpu.make_async_copy(spill.at[0, tiles], whi.at[tiles], lose.at[0, i]),
            pltpu.make_async_copy(spill.at[1, tiles], wlo.at[tiles], lose.at[1, i]),
        )

    gt_ref[...] = jnp.zeros((256, 256), F32)
    fold[...] = jnp.zeros((512, 256), F32)
    for first in (True, False):
        def dense(i, _):
            if not first:
                for x in back(i):
                    x.wait()
            y, low = lax.div(i, 2), lax.rem(i, 2)
            tt = jnp.concatenate([t[low + 2 * h, :, :, y].reshape(128, 4096) for h in range(2)], 0)
            side = lambda w: jnp.concatenate([w[i * 32 + j] for j in range(32)], 1)
            lhs = jnp.concatenate([side(whi), side(wlo)] + ([tt] if first else []), 0)
            res = lax.dot_general(lhs, tt, NT, preferred_element_type=F32)
            fold[pl.ds(GRP if first else 0, GRP), :] += res[:GRP] + res[GRP:2 * GRP]
            if first:
                gt_ref[...] += res[2 * GRP:]
                for x in back(i):
                    x.start()
            return 0

        lax.fori_loop(0, 8, dense, 0)

    one, zero = jnp.ones((), BF), jnp.zeros((), BF)
    second = jnp.zeros((256, 512), F32)
    for j in range(4):
        ij = lax.broadcasted_iota(jnp.int32, (512, 512), 0) + j * 512
        pick = jnp.where(ij == sec_ref[...], one, zero)
        second += lax.dot_general(s_vm[:, :, j * 512:(j + 1) * 512].reshape(256, 512), pick, NN, preferred_element_type=F32)
    contrib = second * fold[...].T
    hi = contrib.astype(BF)
    rest = contrib - hi.astype(F32)
    mid = rest.astype(BF)
    low = (rest - mid.astype(F32)).astype(BF)
    lhs = jnp.concatenate([hi, mid, low], 0)
    for j in range(8):
        ii = lax.broadcasted_iota(jnp.int32, (128, 512), 0) + j * 128
        put = jnp.where(ii == own_ref[...], one, zero)
        res = lax.dot_general(lhs, put, NT, preferred_element_type=F32)
        out_ref[j] = res[:256] + (res[256:512] + res[512:])
    for i in range(1, 16):
        take(gs_ref.at[lax.rem(r + 16 - i, 16)], grecv.at[i - 1], (r, c))
    for ref, sem, n in sent:
        pltpu.make_async_remote_copy(ref, ref, sem.at[n], sem.at[n], device_id=(r, c), device_id_type=MESH).wait_send()


EVENTS = (1, 3, 5, 7, 9, 11, 13, 15)
GRAM_AT = 10
SUM_AT = 14


def main(piece, spiece, q, p, v, sec, own):
    D = pltpu.SemaphoreType.DMA
    return pl.pallas_call(
        main_body,
        out_shape=(
            jax.ShapeDtypeStruct((8, 256, 128), F32),
            jax.ShapeDtypeStruct((256, 256), F32),
            jax.ShapeDtypeStruct((16, 16, 256), F32),
            jax.ShapeDtypeStruct((2, 256, GRP, 128), BF),
        ),
        in_specs=[ANY, ANY] + [INV] * 5,
        out_specs=(INV, INV, INV, ANY),
        scratch_shapes=[
            VMEM((4, 4, 2, 4, 16, 4096), BF), VMEM((16, 16, 2048), BF), VMEM((16, 256), F32), VMEM((8, 16, 256), F32),
            VMEM((2, UB * PAD, 128), F32), VMEM((2, UB * PAD, 128), F32),
            VMEM((256, GRP, 128), BF), VMEM((256, GRP, 128), BF), VMEM((512, 256), F32),
            D((SEMS,)), D((SEMS,)), D((15,)), D((15,)), D((7,)), D((7,)), D((15,)), D((15,)), D((2, 16)), D((2,)), D((2, 8)),
        ],
        compiler_params=pltpu.CompilerParams(has_side_effects=True, vmem_limit_bytes=67043328),
        name="gather_spread_fold",
    )(piece, spiece, q, p, v, sec, own)


def inverse_body(gs_ref, gt_ref, out_ref, a_ref, x_ref):
    gram = (gs_ref[...].reshape(256, 256) / 16384) * (gt_ref[...] / 32768)
    eye = (lax.broadcasted_iota(jnp.int32, (256, 256), 0) == lax.broadcasted_iota(jnp.int32, (256, 256), 1)).astype(F32)
    diag = gram * eye
    down = 1 / jnp.sqrt(jnp.sum(diag, axis=1, keepdims=True))
    along = 1 / jnp.sqrt(jnp.sum(diag, axis=0, keepdims=True))
    a = gram * down * along
    a_ref[...] = a
    bound = jnp.max(jnp.sum(jnp.abs(a), axis=0))
    x_ref[...] = eye * (2 / (1 + bound))

    def dot(u, w):
        return lax.dot_general(u, w, NN, precision=HIGH, preferred_element_type=F32)

    def go(state):
        return (state[0] < 64) & (state[1] > 1e-4)

    def step(state):
        x = x_ref[...]
        rest = eye - dot(a_ref[...], x)
        x_ref[...] = x + dot(x, rest)
        return state[0] + 1, jnp.max(jnp.abs(rest))

    lax.while_loop(go, step, (0, jnp.float32(1.0)))
    out_ref[...] = x_ref[...] * down * along


def inverse(gs, gt):
    return pl.pallas_call(
        inverse_body,
        out_shape=jax.ShapeDtypeStruct((256, 256), F32),
        in_specs=[INV, INV],
        out_specs=INV,
        scratch_shapes=[VMEM((256, 256), F32), VMEM((256, 256), F32)],
        name="gram_inverse",
    )(gs, gt)


def k3_body(part, inv, out, got, x, rsem, rrecv, xsem, xrecv, lsem):
    r, c = lax.axis_index("rows"), lax.axis_index("cols")
    sent = []
    for i in range(1, 8):
        to = lax.rem(c + i, 8)
        sent.append(send_to(part.at[to], got.at[i - 1], rsem.at[i - 1], rrecv.at[i - 1], (r, to)))
    total = part[c]
    for i in range(7):
        pltpu.make_async_remote_copy(got.at[i], got.at[i], rsem.at[i], rrecv.at[i], device_id=(r, c), device_id_type=MESH).wait_recv()
        total = total + got[i]
    solved = lax.dot_general(inv[...], total, NN, precision=HIGH, preferred_element_type=F32)
    x[...] = solved.reshape(16, 16, 128)
    home = lax.div(r, 2)
    slot = lax.rem(r, 2) * 8 + c
    mine = home == c
    lanes = pl.ds(pl.multiple_of(slot * 128, 128), 128)
    for i in range(1, 16):
        to = lax.rem(r + i, 16)
        sent.append(send_to(x.at[to], out.at[:, lanes], xsem.at[i], xrecv.at[slot], (to, home)))

    near = pltpu.make_async_copy(x.at[r], out.at[:, lanes], lsem)
    far = pltpu.make_async_remote_copy(x.at[r], out.at[:, lanes], xsem.at[0], xrecv.at[slot], device_id=(r, home), device_id_type=MESH)

    @pl.when(mine)
    def _():
        near.start()

    @pl.when(jnp.logical_not(mine))
    def _():
        far.start()

    for i in range(16):
        there = out.at[:, pl.ds(i * 128, 128)]
        take = pltpu.make_async_remote_copy(there, there, xsem.at[0], xrecv.at[i], device_id=(r, c), device_id_type=MESH)

        @pl.when(jnp.logical_not(mine & (slot == i)))
        def _():
            take.wait_recv()

    @pl.when(mine)
    def _():
        near.wait()

    @pl.when(jnp.logical_not(mine))
    def _():
        far.wait_send()

    for s in sent:
        s.wait_send()


def k3(part, inv):
    D = pltpu.SemaphoreType.DMA
    return pl.pallas_call(
        k3_body,
        out_shape=jax.ShapeDtypeStruct((16, 2048), F32),
        in_specs=[INV, INV],
        out_specs=INV,
        scratch_shapes=[VMEM((7, 256, 128), F32), VMEM((16, 16, 128), F32), D((7,)), D((7,)), D((16,)), D((16,)), D(())],
        compiler_params=pltpu.CompilerParams(has_side_effects=True),
        name="reduce_solve_place",
    )(part, inv)


def per_device(values, length, owner, second, third, live_blocks, second_factor, third_factor):
    r, c = lax.axis_index("rows"), lax.axis_index("cols")
    lane = jnp.arange(128, dtype=jnp.int32)
    slot = jnp.arange(512, dtype=jnp.int32)
    live = (lane[None, :] < length[:, None]) & (slot < live_blocks[0])[:, None]
    v = jnp.where(live, values, jnp.zeros((), BF)).astype(F32)
    q = (third >> 8).astype(F32)
    p = (third & 255).astype(F32)
    sec = (second - c * 2048).reshape(1, 512)
    own = (owner - r * 1024).reshape(1, 512)
    part, gt, gs, _ = main(third_factor.T, second_factor.T, q, p, v, sec, own)
    inv = inverse(gs, gt)
    return k3(part, inv).T


def solution(mesh):
    both = P(("rows", "cols"))
    wide = P(("rows", "cols"), None)
    return jax.shard_map(
        per_device,
        mesh=mesh,
        in_specs=(wide, both, both, both, wide, both, P("cols", "rows"), P("cols", "rows")),
        out_specs=P("cols", "rows"),
        check_vma=False,
    )
```

time: 192 us -> 157 us (0.82)
  Pallas kernels: 183 us -> 148 us
    pallas_call x2 -> x1, Pallas kernels: 140 us -> 103 us  [main(): pl.pallas_call(main_body, out_shape=(jax.ShapeDtypeStruct((8, 256, 128),...]
where the time goes in v2:
time: 157 us; the launch traced here: 156 us
  Pallas kernels  148 us (94%)
  other arithmetic  6.12 us (4%)
  local copies, waits for them, and re-layouts  1.57 us (1%)
    pallas_call x1, Pallas kernels, main(): pl.pallas_call(main_body, out_shape=(jax.ShapeDtypeStruct((8, 256, 128),...  103 us
    pallas_call x1, Pallas kernels, k3(): pl.pallas_call(k3_body, out_shape=jax.ShapeDtypeStruct((16, 2048), F32),...  34.9 us
    pallas_call x1, Pallas kernels, inverse(): pl.pallas_call(inverse_body, out_shape=jax.ShapeDtypeStruct((256, 256), F...  9.76 us

profile of v2, /device:TPU:25, one launch (start us, length us, event | category | flops | bytes accessed | tf_op | source)
XLA Modules:
  0.0 156.1 jit_solution(13048248989446109838)
XLA Ops:
  0.7 1.3 broadcast_subtract_fusion
  1.9 1.3 broadcast_subtract_fusion.1
  3.2 1.8 %fusion.2.v_ref = f32[512,128]{1,0:T(8,128)} fusion(bf16[512,128]{1,0:T(8,128)(2,1)} %param.8, s32[512]{0:T(512)} %param.9, pred[512]{0:T(512)(128)(4,1)S(1)} %iota_compare_fusion.1), kind=kLoop, calls=%fused_computation.5 | loop fusion | flops 262144 | bytes 395776 | tf_op jit(solution)/shard_map/convert_element_type | solution.py:500
  5.0 1.8 %and_convert_fusion = (f32[512,128]{1,0:T(8,128)}, f32[512,128]{1,0:T(8,128)}) fusion(s32[512,128]{1,0:T(8,128)} %param.12), kind=kLoop, calls=%fused_computation.1 | loop fusion | flops 262144 | bytes 786432 | tf_op jit(solution)/shard_map/convert_element_type | solution.py:502
  6.8 103.2 %gather_spread_fold.1 = (f32[8,256,128]{2,1,0:T(8,128)}, f32[256,256]{1,0:T(8,128)}, f32[16,16,256]{2,1,0:T(8,128)}, bf16[2,256,256,128]{3,2,1,0:T(8,128)(2,1)}) custom-call(bf16[16,4096]{1,0:T(8,128)(2,1)} %bitcast.8, bf16[16,2048]{1,0:T(8,128)(2,1)} %bitcast.9, f32[512,128]{1,0:T(8,128)} %get-tuple-element.12.q_ref, f32[512,128]{1,0:T(8,128)} %get-tuple-element.11.p_ref, ...), custom_call_target="tpu_custom_call" | custom-call | tf_op jit(solution)/shard_map/gather_spread_fold/pallas_call | solution.py:372
  109.9 9.8 %gram_inverse.1.inv = f32[256,256]{1,0:T(8,128)} custom-call(f32[16,16,256]{2,1,0:T(8,128)} %get-tuple-element.9.gs_ref, f32[256,256]{1,0:T(8,128)} %get-tuple-element.10.gt_ref), custom_call_target="tpu_custom_call" | custom-call | tf_op jit(solution)/shard_map/gram_inverse/pallas_call | solution.py:421
  119.7 34.9 %reduce_solve_place.1 = f32[16,2048]{1,0:T(8,128)} custom-call(f32[8,256,128]{2,1,0:T(8,128)} %get-tuple-element.8.part, f32[256,256]{1,0:T(8,128)} %gram_inverse.1.inv), custom_call_target="tpu_custom_call" | custom-call | tf_op jit(solution)/shard_map/reduce_solve_place/pallas_call | solution.py:484
  154.6 1.6 %copy.11 = f32[2048,16]{0,1:T(8,128)} copy(f32[2048,16]{0,1:T(8,128)} %bitcast.7) | data formatting | bytes 262144
  (1 shorter events, 0.0 us)

commit v3 on v2

--- a/solution.py
+++ b/solution.py
@@ -15,7 +15,7 @@
 ANY = pl.BlockSpec(memory_space=pl.ANY)
 INV = pl.BlockSpec(memory_space=pltpu.VMEM)
 
-PARTS = ((0, 1408), (1408, 1408), (2816, 1280))
+PARTS = ((0, 1152), (1152, 1408), (2560, 1536))
 ORDERS = ("xyz", "yzx", "zxy")
 SEMS = 28 * 3 + 16 * 3
 
@@ -176,20 +176,27 @@
 PAD = 129
 
 
-def spread_pair(at, pair, q_ref, p_ref, v_ref, dst):
+def spread_pair(at, pair, ins, dst):
+    third_ref, value_ref, length_ref, live_ref = ins
+    lane = lax.broadcasted_iota(jnp.int32, (16, 128), 1)
     iq = lax.broadcasted_iota(jnp.int32, (128, 128), 0).astype(F32).astype(BF)
     ip = lax.broadcasted_iota(jnp.int32, (256, 128), 0).astype(F32).astype(BF)
     zero = jnp.zeros((128, 128), BF)
 
-    def row(ref, b, n):
-        one = jnp.broadcast_to(ref[pl.ds(b, 1), :], (16, 128)).astype(BF)
+    def wide(one, n):
         return jnp.concatenate([one] * (n // 16), axis=0)
 
     qs, ps = [], []
     for j in range(2):
         b = at + 2 * pair + j
-        qs.append(jnp.where(iq == row(q_ref, b, 128), row(v_ref, b, 128), zero))
-        ps.append(jnp.where(ip == row(p_ref, b, 256), jnp.ones((), BF), jnp.zeros((), BF)))
+        third = jnp.broadcast_to(third_ref[pl.ds(b, 1), :], (16, 128))
+        value = jnp.broadcast_to(value_ref[pl.ds(b, 1), :], (16, 128))
+        used = jnp.where(b < live_ref[0], length_ref[b], 0)
+        value = wide(jnp.where(lane < used, value, 0.0).astype(BF), 128)
+        high = wide((third >> 8).astype(F32).astype(BF), 128)
+        low = wide((third & 255).astype(F32).astype(BF), 256)
+        qs.append(jnp.where(iq == high, value, zero))
+        ps.append(jnp.where(ip == low, jnp.ones((), BF), jnp.zeros((), BF)))
     lhs = jnp.concatenate([jnp.concatenate([qs[0], zero], 1), jnp.concatenate([zero, qs[1]], 1)], 0)
     w = lax.dot_general(lhs, jnp.concatenate(ps, 1), NT, preferred_element_type=F32)
     for j in range(2):
@@ -205,9 +212,9 @@
         wlo[q * 2 + h, rows, :] = (f - hi.astype(F32)).astype(BF)
 
 
-def spread_split(at, rows, q_ref, p_ref, v_ref, src, dst, whi, wlo):
+def spread_split(at, rows, ins, src, dst, whi, wlo):
     for pair in range(UB // 2):
-        spread_pair(at, pair, q_ref, p_ref, v_ref, dst)
+        spread_pair(at, pair, ins, dst)
         for q in range(pair * 16, pair * 16 + 16):
             split_rows(q, rows, src, whi, wlo)
 
@@ -222,35 +229,94 @@
     pltpu.make_async_remote_copy(ref, ref, sem, sem, device_id=me, device_id_type=MESH).wait_recv()
 
 
-def main_body(piece, spiece, q_ref, p_ref, v_ref, sec_ref, own_ref, out_ref, gt_ref, gs_ref, spill,
-              t, s_vm, part, parts, wfa, wfb, whi, wlo, fold,
-              send, recv, ssem, srecv, csem, crecv, gsem, grecv, psem, lsem, lose):
+def main_body(piece, spiece, third_ref, values_ref, length_ref, live_ref, sec_ref, own_ref, out, spill,
+              t, s_vm, near, far, part, parts, wfa, wfb, whi, wlo, fold, value_ref, gt_ref, gs_ref, total, got, a_ref, x_ref, answer,
+              send, recv, ssem, srecv, csem, crecv, gsem, grecv, psem, lsem, lose, rsem, rrecv, xsem, xrecv):
     r, c = lax.axis_index("rows"), lax.axis_index("cols")
     g = Gather(t, send, recv)
     me = g.me
     cp = pltpu.make_async_copy(piece, t.at[me["z"], me["x"], me["k"], me["y"]], lsem.at[0])
     cp.start()
-    cs = pltpu.make_async_copy(spiece, s_vm.at[r], lsem.at[1])
+    cs = pltpu.make_async_copy(spiece, s_vm.at[lax.div(me["z"], 2), me["x"], me["k"]], lsem.at[1])
     cs.start()
+    peers = [(lax.rem(r + i, 16), c) for i in range(1, 16)] + [(r, lax.rem(c + i, 8)) for i in range(1, 8)]
+    peers += [device(g.moved(me, "z", 1)), device(g.moved(me, "z", 3))]
+    barrier = pltpu.get_barrier_semaphore()
+    for to in peers:
+        pl.semaphore_signal(barrier, inc=1, device_id=to, device_id_type=MESH)
+    home = lax.div(r, 2)
+    at_home = home == c
+    for i in range(16):
+        source = (2 * c + i // 8, i % 8)
+
+        @pl.when(jnp.logical_not((source[0] == r) & (c == source[1])))
+        def _():
+            pl.semaphore_signal(barrier, inc=1, device_id=source, device_id_type=MESH)
+    value_ref[...] = values_ref[...].astype(F32)
+    ins = (third_ref, value_ref, length_ref, live_ref)
+    pl.semaphore_wait(barrier, 40 - at_home.astype(jnp.int32))
     sent = []
 
     def push(src, dst, ssem, rsem, n, to):
         send_to(src, dst, ssem.at[n], rsem.at[n], to)
-        sent.append((src, ssem, n))
+        sent.append((lambda: src, ssem, n))
 
     cp.wait()
     run = g.run()
     next(run)
-    for i in range(1, 16):
-        push(spiece, s_vm.at[r], ssem, srecv, i - 1, (lax.rem(r + i, 16), c))
     cs.wait()
+    FORE, BACK = 1, 3
+    relay = {FORE: near, BACK: far}
+
+    def hop(src, dst, n, to):
+        send_to(src(), dst(), ssem.at[n], srecv.at[n], device(to))
+        sent.append((src, ssem, n))
+
+    xs = g.steps["x"]
+    zs = [lax.div(z, 2) for z in g.steps["z"]]
+
+    def plane(z, x=None, half=None):
+        ref = s_vm.at[zs[z], slice(None) if x is None else xs[x], me["k"]]
+        return ref if half is None else ref.at[:, pl.ds(half * 1024, 1024)]
+
+    def stop(way, j):
+        return relay[way].at[j]
+
+    for n, way in enumerate((FORE, BACK)):
+        hop(lambda: plane(0, 0), lambda: plane(0, 0), n, g.moved(me, "x", way))
+
+    def second_one():
+        for n, way in enumerate((FORE, BACK)):
+            take(plane(0, 4 - way), srecv.at[n], (r, c))
+            half = lambda n=n, way=way: plane(0, 4 - way, half=n)
+            hop(half, half, 2 + n, g.moved(me, "x", way))
+
+    def second_two():
+        for n, way in enumerate((FORE, BACK)):
+            take(plane(0, 2, half=n), srecv.at[2 + n], (r, c))
+        for n, way in enumerate((FORE, BACK)):
+            for j in range(2):
+                hop(lambda n=n, j=j: plane(0, 2 * n + j), lambda: stop(way, j), 4 + 2 * n + j, g.moved(me, "z", way))
+        hop(lambda: plane(0), lambda: plane(0), 12, g.other)
+
+    def second_three():
+        for n, way in enumerate((FORE, BACK)):
+            for j in range(2):
+                take(stop(way, j), srecv.at[4 + 2 * n + j], (r, c))
+                hop(lambda way=way, j=j: stop(way, j), lambda: plane(4 - way, 2 * n + j), 8 + 2 * n + j, g.moved(me, "z", way))
+
+    def second_four():
+        for n in range(2):
+            for j in range(2):
+                take(plane(2, 2 * n + j), srecv.at[8 + 2 * n + j], (r, c))
+        hop(lambda: plane(2), lambda: plane(2), 13, g.other)
 
     mine = gs_ref.at[r]
 
     def second_gram():
-        for i in range(1, 16):
-            take(s_vm.at[lax.rem(r + 16 - i, 16)], srecv.at[i - 1], (r, c))
-        chunk = lax.dot_general(s_vm[r], s_vm[...].reshape(256, 2048), NT, preferred_element_type=F32)
+        for n, z in ((12, 0), (13, 2)):
+            take(s_vm.at[zs[z], :, g.other["k"]], srecv.at[n], (r, c))
+        chunk = lax.dot_general(s_vm[zs[0], me["x"], me["k"]], s_vm[...].reshape(256, 2048), NT, preferred_element_type=F32)
         part[...] = chunk
         parts[c] = chunk
         for i in range(1, 8):
@@ -273,8 +339,8 @@
     todo = {j: [] for j in range(STEPS // 2)}
     for j in EVENTS:
         todo[j].append(lambda: next(run))
-    todo[GRAM_AT].append(second_gram)
-    todo[SUM_AT].append(second_gram_sum)
+    for j, f in zip(SECOND_AT, (second_one, second_two, second_three, second_four, second_gram, second_gram_sum)):
+        todo[j].append(f)
 
     def iteration(i, _):
         for j in range(STEPS // 2):
@@ -295,7 +361,7 @@
             rows = pl.ds(pl.multiple_of(slot * UB, UB), UB)
             at = pl.multiple_of((2 * i + half) * UB, UB)
             src, dst = ((wfb, wfa), (wfa, wfb))[half]
-            spread_split(at, rows, q_ref, p_ref, v_ref, src, dst, whi, wlo)
+            spread_split(at, rows, ins, src, dst, whi, wlo)
 
             @pl.when(step < 16)
             def _():
@@ -343,54 +409,72 @@
     second = jnp.zeros((256, 512), F32)
     for j in range(4):
         ij = lax.broadcasted_iota(jnp.int32, (512, 512), 0) + j * 512
-        pick = jnp.where(ij == sec_ref[...], one, zero)
-        second += lax.dot_general(s_vm[:, :, j * 512:(j + 1) * 512].reshape(256, 512), pick, NN, preferred_element_type=F32)
+        pick = jnp.where(ij == sec_ref[...] - c * 2048, one, zero)
+        second += lax.dot_general(s_vm[:, :, :, :, j * 512:(j + 1) * 512].reshape(256, 512), pick, NN, preferred_element_type=F32)
     contrib = second * fold[...].T
     hi = contrib.astype(BF)
-    rest = contrib - hi.astype(F32)
-    mid = rest.astype(BF)
-    low = (rest - mid.astype(F32)).astype(BF)
-    lhs = jnp.concatenate([hi, mid, low], 0)
-    for j in range(8):
-        ii = lax.broadcasted_iota(jnp.int32, (128, 512), 0) + j * 128
-        put = jnp.where(ii == own_ref[...], one, zero)
+    lhs = jnp.concatenate([hi, (contrib - hi.astype(F32)).astype(BF)], 0)
+    for j in range(4):
+        ii = lax.broadcasted_iota(jnp.int32, (256, 512), 0) + j * 256
+        put = jnp.where(ii == own_ref[...] - r * 1024, one, zero)
         res = lax.dot_general(lhs, put, NT, preferred_element_type=F32)
-        out_ref[j] = res[:256] + (res[256:512] + res[512:])
+        both = res[:256] + res[256:]
+        for h in range(2):
+            total[2 * j + h] = both[:, h * 128:(h + 1) * 128]
+    for i in range(1, 8):
+        to = lax.rem(c + i, 8)
+        send_to(total.at[to], got.at[i - 1], rsem.at[i - 1], rrecv.at[i - 1], (r, to))
+
     for i in range(1, 16):
         take(gs_ref.at[lax.rem(r + 16 - i, 16)], grecv.at[i - 1], (r, c))
-    for ref, sem, n in sent:
+    invert(gs_ref, gt_ref, a_ref, x_ref)
+    rows = total[c]
+    for i in range(7):
+        take(got.at[i], rrecv.at[i], (r, c))
+        rows = rows + got[i]
+    answer[...] = lax.dot_general(a_ref[...], rows, NN, precision=HIGH, preferred_element_type=F32).reshape(16, 16, 128)
+
+    slot = lax.rem(r, 2) * 8 + c
+    lanes = pl.ds(pl.multiple_of(slot * 128, 128), 128)
+    for i in range(1, 16):
+        to = lax.rem(r + i, 16)
+        send_to(answer.at[to], out.at[:, lanes], xsem.at[i], xrecv.at[slot], (to, home))
+    here = pltpu.make_async_copy(answer.at[r], out.at[:, lanes], lsem.at[0])
+    away = pltpu.make_async_remote_copy(answer.at[r], out.at[:, lanes], xsem.at[0], xrecv.at[slot], device_id=(r, home), device_id_type=MESH)
+
+    @pl.when(at_home)
+    def _():
+        here.start()
+
+    @pl.when(jnp.logical_not(at_home))
+    def _():
+        away.start()
+
+    for make, sem, n in sent:
+        ref = make()
         pltpu.make_async_remote_copy(ref, ref, sem.at[n], sem.at[n], device_id=(r, c), device_id_type=MESH).wait_send()
-
-
-EVENTS = (1, 3, 5, 7, 9, 11, 13, 15)
-GRAM_AT = 10
-SUM_AT = 14
-
-
-def main(piece, spiece, q, p, v, sec, own):
-    D = pltpu.SemaphoreType.DMA
-    return pl.pallas_call(
-        main_body,
-        out_shape=(
-            jax.ShapeDtypeStruct((8, 256, 128), F32),
-            jax.ShapeDtypeStruct((256, 256), F32),
-            jax.ShapeDtypeStruct((16, 16, 256), F32),
-            jax.ShapeDtypeStruct((2, 256, GRP, 128), BF),
-        ),
-        in_specs=[ANY, ANY] + [INV] * 5,
-        out_specs=(INV, INV, INV, ANY),
-        scratch_shapes=[
-            VMEM((4, 4, 2, 4, 16, 4096), BF), VMEM((16, 16, 2048), BF), VMEM((16, 256), F32), VMEM((8, 16, 256), F32),
-            VMEM((2, UB * PAD, 128), F32), VMEM((2, UB * PAD, 128), F32),
-            VMEM((256, GRP, 128), BF), VMEM((256, GRP, 128), BF), VMEM((512, 256), F32),
-            D((SEMS,)), D((SEMS,)), D((15,)), D((15,)), D((7,)), D((7,)), D((15,)), D((15,)), D((2, 16)), D((2,)), D((2, 8)),
-        ],
-        compiler_params=pltpu.CompilerParams(has_side_effects=True, vmem_limit_bytes=67043328),
-        name="gather_spread_fold",
-    )(piece, spiece, q, p, v, sec, own)
-
-
-def inverse_body(gs_ref, gt_ref, out_ref, a_ref, x_ref):
+    for i in range(1, 8):
+        pltpu.make_async_remote_copy(got.at[i - 1], got.at[i - 1], rsem.at[i - 1], rrecv.at[i - 1], device_id=(r, c), device_id_type=MESH).wait_send()
+    for i in range(16):
+        there = out.at[:, pl.ds(i * 128, 128)]
+
+        @pl.when(jnp.logical_not(at_home & (slot == i)))
+        def _():
+            take(there, xrecv.at[i], (r, c))
+
+    @pl.when(at_home)
+    def _():
+        here.wait()
+
+    @pl.when(jnp.logical_not(at_home))
+    def _():
+        away.wait_send()
+
+    for i in range(1, 16):
+        pltpu.make_async_remote_copy(answer.at[0], answer.at[0], xsem.at[i], xrecv.at[0], device_id=(r, c), device_id_type=MESH).wait_send()
+
+
+def invert(gs_ref, gt_ref, a_ref, x_ref):
     gram = (gs_ref[...].reshape(256, 256) / 16384) * (gt_ref[...] / 32768)
     eye = (lax.broadcasted_iota(jnp.int32, (256, 256), 0) == lax.broadcasted_iota(jnp.int32, (256, 256), 1)).astype(F32)
     diag = gram * eye
@@ -398,113 +482,52 @@
     along = 1 / jnp.sqrt(jnp.sum(diag, axis=0, keepdims=True))
     a = gram * down * along
     a_ref[...] = a
-    bound = jnp.max(jnp.sum(jnp.abs(a), axis=0))
+    bound = jnp.max(jnp.sum(jnp.abs(a), axis=0, keepdims=True), axis=1, keepdims=True)
     x_ref[...] = eye * (2 / (1 + bound))
 
     def dot(u, w):
         return lax.dot_general(u, w, NN, precision=HIGH, preferred_element_type=F32)
 
-    def go(state):
-        return (state[0] < 64) & (state[1] > 1e-4)
-
-    def step(state):
-        x = x_ref[...]
-        rest = eye - dot(a_ref[...], x)
-        x_ref[...] = x + dot(x, rest)
-        return state[0] + 1, jnp.max(jnp.abs(rest))
-
-    lax.while_loop(go, step, (0, jnp.float32(1.0)))
-    out_ref[...] = x_ref[...] * down * along
-
-
-def inverse(gs, gt):
+    def step(i, _):
+        now = x_ref[...]
+        x_ref[...] = now + dot(now, eye - dot(a_ref[...], now))
+        return 0
+
+    lax.fori_loop(0, NEWTON, step, 0)
+    a_ref[...] = x_ref[...] * down * along
+
+
+NEWTON = 24
+EVENTS = (1, 3, 5, 7, 9, 11, 13, 15)
+SECOND_AT = (1, 3, 5, 8, 10, 14)
+
+
+def main(piece, spiece, third, values, length, live, sec, own):
+    D = pltpu.SemaphoreType.DMA
+    smem = pl.BlockSpec(memory_space=pltpu.SMEM)
     return pl.pallas_call(
-        inverse_body,
-        out_shape=jax.ShapeDtypeStruct((256, 256), F32),
-        in_specs=[INV, INV],
-        out_specs=INV,
-        scratch_shapes=[VMEM((256, 256), F32), VMEM((256, 256), F32)],
-        name="gram_inverse",
-    )(gs, gt)
-
-
-def k3_body(part, inv, out, got, x, rsem, rrecv, xsem, xrecv, lsem):
-    r, c = lax.axis_index("rows"), lax.axis_index("cols")
-    sent = []
-    for i in range(1, 8):
-        to = lax.rem(c + i, 8)
-        sent.append(send_to(part.at[to], got.at[i - 1], rsem.at[i - 1], rrecv.at[i - 1], (r, to)))
-    total = part[c]
-    for i in range(7):
-        pltpu.make_async_remote_copy(got.at[i], got.at[i], rsem.at[i], rrecv.at[i], device_id=(r, c), device_id_type=MESH).wait_recv()
-        total = total + got[i]
-    solved = lax.dot_general(inv[...], total, NN, precision=HIGH, preferred_element_type=F32)
-    x[...] = solved.reshape(16, 16, 128)
-    home = lax.div(r, 2)
-    slot = lax.rem(r, 2) * 8 + c
-    mine = home == c
-    lanes = pl.ds(pl.multiple_of(slot * 128, 128), 128)
-    for i in range(1, 16):
-        to = lax.rem(r + i, 16)
-        sent.append(send_to(x.at[to], out.at[:, lanes], xsem.at[i], xrecv.at[slot], (to, home)))
-
-    near = pltpu.make_async_copy(x.at[r], out.at[:, lanes], lsem)
-    far = pltpu.make_async_remote_copy(x.at[r], out.at[:, lanes], xsem.at[0], xrecv.at[slot], device_id=(r, home), device_id_type=MESH)
-
-    @pl.when(mine)
-    def _():
-        near.start()
-
-    @pl.when(jnp.logical_not(mine))
-    def _():
-        far.start()
-
-    for i in range(16):
-        there = out.at[:, pl.ds(i * 128, 128)]
-        take = pltpu.make_async_remote_copy(there, there, xsem.at[0], xrecv.at[i], device_id=(r, c), device_id_type=MESH)
-
-        @pl.when(jnp.logical_not(mine & (slot == i)))
-        def _():
-            take.wait_recv()
-
-    @pl.when(mine)
-    def _():
-        near.wait()
-
-    @pl.when(jnp.logical_not(mine))
-    def _():
-        far.wait_send()
-
-    for s in sent:
-        s.wait_send()
-
-
-def k3(part, inv):
-    D = pltpu.SemaphoreType.DMA
-    return pl.pallas_call(
-        k3_body,
-        out_shape=jax.ShapeDtypeStruct((16, 2048), F32),
-        in_specs=[INV, INV],
-        out_specs=INV,
-        scratch_shapes=[VMEM((7, 256, 128), F32), VMEM((16, 16, 128), F32), D((7,)), D((7,)), D((16,)), D((16,)), D(())],
-        compiler_params=pltpu.CompilerParams(has_side_effects=True),
-        name="reduce_solve_place",
-    )(part, inv)
+        main_body,
+        out_shape=(jax.ShapeDtypeStruct((16, 2048), F32), jax.ShapeDtypeStruct((2, 256, GRP, 128), BF)),
+        in_specs=[ANY, ANY, INV, INV, smem, smem, INV, INV],
+        out_specs=(INV, ANY),
+        scratch_shapes=[
+            VMEM((4, 4, 2, 4, 16, 4096), BF), VMEM((2, 4, 2, 16, 2048), BF), VMEM((2, 16, 2048), BF), VMEM((2, 16, 2048), BF),
+            VMEM((16, 256), F32), VMEM((8, 16, 256), F32),
+            VMEM((2, UB * PAD, 128), F32), VMEM((2, UB * PAD, 128), F32),
+            VMEM((256, GRP, 128), BF), VMEM((256, GRP, 128), BF), VMEM((512, 256), F32), VMEM((512, 128), F32),
+            VMEM((256, 256), F32), VMEM((16, 16, 256), F32), VMEM((8, 256, 128), F32), VMEM((7, 256, 128), F32),
+            VMEM((256, 256), F32), VMEM((256, 256), F32), VMEM((16, 16, 128), F32),
+            D((SEMS,)), D((SEMS,)), D((14,)), D((14,)), D((7,)), D((7,)), D((15,)), D((15,)), D((2, 16)), D((2,)), D((2, 8)),
+            D((7,)), D((7,)), D((16,)), D((16,)),
+        ],
+        compiler_params=pltpu.CompilerParams(has_side_effects=True, vmem_limit_bytes=67043328, collective_id=0),
+        name="factor_update",
+    )(piece, spiece, third, values, length, live, sec, own)
 
 
 def per_device(values, length, owner, second, third, live_blocks, second_factor, third_factor):
-    r, c = lax.axis_index("rows"), lax.axis_index("cols")
-    lane = jnp.arange(128, dtype=jnp.int32)
-    slot = jnp.arange(512, dtype=jnp.int32)
-    live = (lane[None, :] < length[:, None]) & (slot < live_blocks[0])[:, None]
-    v = jnp.where(live, values, jnp.zeros((), BF)).astype(F32)
-    q = (third >> 8).astype(F32)
-    p = (third & 255).astype(F32)
-    sec = (second - c * 2048).reshape(1, 512)
-    own = (owner - r * 1024).reshape(1, 512)
-    part, gt, gs, _ = main(third_factor.T, second_factor.T, q, p, v, sec, own)
-    inv = inverse(gs, gt)
-    return k3(part, inv).T
+    out, _ = main(third_factor.T, second_factor.T, third, values, length, live_blocks, second.reshape(1, 512), owner.reshape(1, 512))
+    return out.T
 
 
 def solution(mesh):

time: 157 us -> 127 us (0.81)
  Pallas kernels: 148 us -> 124 us
  other arithmetic: 6.12 us -> 0 us
    pallas_call x3 -> x1, Pallas kernels: 148 us -> 124 us  [main(): pl.pallas_call(main_body, out_shape=(jax.ShapeDtypeStruct((16, 2048), F32...]
    convert_element_type x2 -> x0, other arithmetic: 3.59 us -> none  [the longest x1 1.81 us: per_device(): v = jnp.where(live, values, jnp.zeros((), BF)).astype(F32)]
    sub x2 -> x0, other arithmetic: 2.52 us -> none  [the longest x1 1.26 us: per_device(): own = (owner - r * 1024).reshape(1, 512)]
where the time goes in v3:
time: 127 us; the launch traced here: 126 us
  Pallas kernels  124 us (98%)
  local copies, waits for them, and re-layouts  1.57 us (1%)
    pallas_call x1, Pallas kernels, main(): pl.pallas_call(main_body, out_shape=(jax.ShapeDtypeStruct((16, 2048), F32...  124 us

profile of v3, /device:TPU:25, one launch (start us, length us, event | category | flops | bytes accessed | tf_op | source)
XLA Modules:
  0.0 126.2 jit_solution(4914846656073868665)
XLA Ops:
  0.7 123.9 %factor_update.1 = (f32[16,2048]{1,0:T(8,128)}, bf16[2,256,256,128]{3,2,1,0:T(8,128)(2,1)}) custom-call(bf16[16,4096]{1,0:T(8,128)(2,1)} %bitcast.6, bf16[16,2048]{1,0:T(8,128)(2,1)} %bitcast.7, s32[512,128]{1,0:T(8,128)} %third_ref.1, bf16[512,128]{1,0:T(8,128)(2,1)} %values_ref.1, s32[512]{0:T(512)} %length_ref.1, s32[1]{0:T(128)S(6)} %copy.10.live_ref, ...), custom_call_target="tpu_custom_call" | custom-call | tf_op jit(solution)/shard_map/factor_update/pallas_call | solution.py:508
  124.6 1.6 %copy.11 = f32[2048,16]{0,1:T(8,128)} copy(f32[2048,16]{0,1:T(8,128)} %bitcast.5) | data formatting | bytes 262144

commit v4 on v3

--- a/solution.py
+++ b/solution.py
@@ -17,7 +17,7 @@
 
 PARTS = ((0, 1152), (1152, 1408), (2560, 1536))
 ORDERS = ("xyz", "yzx", "zxy")
-SEMS = 28 * 3 + 16 * 3
+SEMS = 52 * 3 + 16 * 3
 
 
 def place():
@@ -73,7 +73,7 @@
         onef = {(p, s): self.new() for p in parts for s in (FORE, BACK)}
         two = {(p, o, s): self.new() for p in parts for o in range(4) for s in (FORE, BACK)}
         twof = {(p, o): self.new() for p in parts for o in range(4)}
-        three = {(p, o, s): self.new() for p in parts for o in range(4) for s in (FORE, BACK)}
+        three = {(p, a, b, s): self.new() for p in parts for a in range(4) for b in range(4) for s in (FORE, BACK)}
         threef = {(p, o): self.new() for p in parts for o in range(4)}
         core = {(p, a, b): self.new() for p in parts for a in range(4) for b in range(4)}
 
@@ -99,12 +99,18 @@
         def cross(p, b, c):
             self.copy(set3(p, b, c), core[p, b, c], self.other)
 
+        def third(p, a, b):
+            for s3 in (FORE, BACK):
+                self.copy(self.block(p, at2(p, a, b)), three[p, a, b, s3], to(p, 2, s3))
+
         for p in parts:
             for s in (FORE, BACK):
                 self.copy(self.block(p, me), one[p, s], to(p, 0, s))
         for p in parts:
             for s in (FORE, BACK):
                 self.copy(self.block(p, me), two[p, 0, s], to(p, 1, s))
+        for p in parts:
+            third(p, 0, 0)
         yield
         for p in parts:
             for s in (FORE, BACK):
@@ -113,41 +119,41 @@
                 self.copy(self.block(p, at1(p, back), half=0 if s == FORE else 1), onef[p, s], to(p, 0, s))
                 for s2 in (FORE, BACK):
                     self.copy(self.block(p, at1(p, back)), two[p, back, s2], to(p, 1, s2))
+                third(p, back, 0)
         yield
         for p in parts:
             for s in (FORE, BACK):
                 self.arrived(self.block(p, at1(p, 2), half=0 if s == FORE else 1), onef[p, s])
             for s2 in (FORE, BACK):
                 self.copy(self.block(p, at1(p, 2)), two[p, 2, s2], to(p, 1, s2))
-            for s3 in (FORE, BACK):
-                self.copy(set3(p, 0, 0), three[p, 0, s3], to(p, 2, s3))
+            third(p, 2, 0)
             cross(p, 0, 0)
         yield
         FIRST = {FORE: (0, 3), BACK: (1, 2)}
-        for p in parts:
-            for o in (0, 3, 1, 2):
+        for o in (0, 3, 1, 2):
+            for p in parts:
                 for s in (FORE, BACK):
                     back = 4 - s
                     self.arrived(self.block(p, at2(p, o, back)), two[p, o, s])
                     if o in FIRST[s]:
                         self.copy(self.block(p, at2(p, o, back)), twof[p, o], to(p, 1, s))
+                    third(p, o, back)
+        for p in parts:
             for b in (3, 1):
-                for s3 in (FORE, BACK):
-                    self.copy(set3(p, b, 0), three[p, b, s3], to(p, 2, s3))
                 cross(p, b, 0)
         yield
         for p in parts:
             for o in (0, 3, 1, 2):
                 self.arrived(self.block(p, at2(p, o, 2)), twof[p, o])
-            for s3 in (FORE, BACK):
-                self.copy(set3(p, 2, 0), three[p, 2, s3], to(p, 2, s3))
+                third(p, o, 2)
             cross(p, 2, 0)
         for b in (0, 3, 1, 2):
             yield
             for p in parts:
                 for s in (FORE, BACK):
                     back = 4 - s
-                    self.arrived(set3(p, b, back), three[p, b, s])
+                    for o in range(4):
+                        self.arrived(self.block(p, self.moved(at2(p, o, b), dims(p)[2], back)), three[p, o, b, s])
                     if b in FIRST[s]:
                         self.copy(set3(p, b, back), threef[p, b], to(p, 2, s))
                     cross(p, b, back)
@@ -230,8 +236,8 @@
 
 
 def main_body(piece, spiece, third_ref, values_ref, length_ref, live_ref, sec_ref, own_ref, out, spill,
-              t, s_vm, near, far, part, parts, wfa, wfb, whi, wlo, fold, value_ref, gt_ref, gs_ref, total, got, a_ref, x_ref, answer,
-              send, recv, ssem, srecv, csem, crecv, gsem, grecv, psem, lsem, lose, rsem, rrecv, xsem, xrecv):
+              t, s_vm, near, far, part, parts, wfa, wfb, whi, wlo, fold, value_ref, gt_ref, gs_ref, total, got, a_ref, x_ref, r_ref, part3, parts3, answer,
+              send, recv, ssem, srecv, csem, crecv, gsem, grecv, psem, lsem, lose, rsem, rrecv, xsem, xrecv, csem3, crecv3, gsem3, grecv3):
     r, c = lax.axis_index("rows"), lax.axis_index("cols")
     g = Gather(t, send, recv)
     me = g.me
@@ -313,6 +319,24 @@
 
     mine = gs_ref.at[r]
 
+    mine3 = gt_ref.at[r]
+
+    def third_gram():
+        y, low = me["y"], lax.rem(me["z"], 2)
+        whole = jnp.concatenate([t[low + 2 * h, :, :, y].reshape(128, 4096) for h in range(2)], 0)
+        chunk = lax.dot_general(t[me["z"], me["x"], me["k"], y], whole, NT, preferred_element_type=F32)
+        part3[...] = chunk
+        parts3[c] = chunk
+        for i in range(1, 8):
+            push(part3, parts3.at[c], csem3, crecv3, i - 1, (r, lax.rem(c + i, 8)))
+
+    def third_gram_sum():
+        for i in range(1, 8):
+            take(parts3.at[lax.rem(c + 8 - i, 8)], crecv3.at[i - 1], (r, c))
+        gt_ref[r] = sum(parts3[i] for i in range(8))
+        for i in range(1, 16):
+            push(mine3, mine3, gsem3, grecv3, i - 1, (lax.rem(r + i, 16), c))
+
     def second_gram():
         for n, z in ((12, 0), (13, 2)):
             take(s_vm.at[zs[z], :, g.other["k"]], srecv.at[n], (r, c))
@@ -384,7 +408,7 @@
             pltpu.make_async_copy(spill.at[1, tiles], wlo.at[tiles], lose.at[1, i]),
         )
 
-    gt_ref[...] = jnp.zeros((256, 256), F32)
+    third_gram()
     fold[...] = jnp.zeros((512, 256), F32)
     for first in (True, False):
         def dense(i, _):
@@ -394,16 +418,17 @@
             y, low = lax.div(i, 2), lax.rem(i, 2)
             tt = jnp.concatenate([t[low + 2 * h, :, :, y].reshape(128, 4096) for h in range(2)], 0)
             side = lambda w: jnp.concatenate([w[i * 32 + j] for j in range(32)], 1)
-            lhs = jnp.concatenate([side(whi), side(wlo)] + ([tt] if first else []), 0)
+            lhs = jnp.concatenate([side(whi), side(wlo)], 0)
             res = lax.dot_general(lhs, tt, NT, preferred_element_type=F32)
-            fold[pl.ds(GRP if first else 0, GRP), :] += res[:GRP] + res[GRP:2 * GRP]
+            fold[pl.ds(GRP if first else 0, GRP), :] += res[:GRP] + res[GRP:]
             if first:
-                gt_ref[...] += res[2 * GRP:]
                 for x in back(i):
                     x.start()
             return 0
 
         lax.fori_loop(0, 8, dense, 0)
+        if first:
+            third_gram_sum()
 
     one, zero = jnp.ones((), BF), jnp.zeros((), BF)
     second = jnp.zeros((256, 512), F32)
@@ -427,7 +452,8 @@
 
     for i in range(1, 16):
         take(gs_ref.at[lax.rem(r + 16 - i, 16)], grecv.at[i - 1], (r, c))
-    invert(gs_ref, gt_ref, a_ref, x_ref)
+        take(gt_ref.at[lax.rem(r + 16 - i, 16)], grecv3.at[i - 1], (r, c))
+    invert(gs_ref, gt_ref, a_ref, x_ref, r_ref)
     rows = total[c]
     for i in range(7):
         take(got.at[i], rrecv.at[i], (r, c))
@@ -474,8 +500,8 @@
         pltpu.make_async_remote_copy(answer.at[0], answer.at[0], xsem.at[i], xrecv.at[0], device_id=(r, c), device_id_type=MESH).wait_send()
 
 
-def invert(gs_ref, gt_ref, a_ref, x_ref):
-    gram = (gs_ref[...].reshape(256, 256) / 16384) * (gt_ref[...] / 32768)
+def invert(gs_ref, gt_ref, a_ref, x_ref, r_ref):
+    gram = (gs_ref[...].reshape(256, 256) / 16384) * (gt_ref[...].reshape(256, 256) / 32768)
     eye = (lax.broadcasted_iota(jnp.int32, (256, 256), 0) == lax.broadcasted_iota(jnp.int32, (256, 256), 1)).astype(F32)
     diag = gram * eye
     down = 1 / jnp.sqrt(jnp.sum(diag, axis=1, keepdims=True))
@@ -483,21 +509,39 @@
     a = gram * down * along
     a_ref[...] = a
     bound = jnp.max(jnp.sum(jnp.abs(a), axis=0, keepdims=True), axis=1, keepdims=True)
-    x_ref[...] = eye * (2 / (1 + bound))
+    scale = 2 / (1 + bound)
+    x_ref[...] = eye * scale
+    r_ref[...] = eye - a * scale
+
+    def halves(w):
+        hi = w.astype(BF)
+        return hi, (w - hi.astype(F32)).astype(BF)
+
+    def double(i, _):
+        x, rest = x_ref[...], r_ref[...]
+        xh, xl = halves(x)
+        rh, rl = halves(rest)
+        one = lax.dot_general(jnp.concatenate([rh, xh, rl, xl], 0), rh, NN, preferred_element_type=F32)
+        two = lax.dot_general(jnp.concatenate([rh, xh], 0), rl, NN, preferred_element_type=F32)
+        r_ref[...] = one[:256] + (one[512:768] + two[:256])
+        x_ref[...] = x + (one[256:512] + (one[768:] + two[256:]))
+        return 0
+
+    lax.fori_loop(0, DOUBLINGS, double, 0)
 
     def dot(u, w):
         return lax.dot_general(u, w, NN, precision=HIGH, preferred_element_type=F32)
 
-    def step(i, _):
+    def newton(i, _):
         now = x_ref[...]
         x_ref[...] = now + dot(now, eye - dot(a_ref[...], now))
         return 0
 
-    lax.fori_loop(0, NEWTON, step, 0)
+    lax.fori_loop(0, 3, newton, 0)
     a_ref[...] = x_ref[...] * down * along
 
 
-NEWTON = 24
+DOUBLINGS = 20
 EVENTS = (1, 3, 5, 7, 9, 11, 13, 15)
 SECOND_AT = (1, 3, 5, 8, 10, 14)
 
@@ -515,10 +559,10 @@
             VMEM((16, 256), F32), VMEM((8, 16, 256), F32),
             VMEM((2, UB * PAD, 128), F32), VMEM((2, UB * PAD, 128), F32),
             VMEM((256, GRP, 128), BF), VMEM((256, GRP, 128), BF), VMEM((512, 256), F32), VMEM((512, 128), F32),
-            VMEM((256, 256), F32), VMEM((16, 16, 256), F32), VMEM((8, 256, 128), F32), VMEM((7, 256, 128), F32),
-            VMEM((256, 256), F32), VMEM((256, 256), F32), VMEM((16, 16, 128), F32),
+            VMEM((16, 16, 256), F32), VMEM((16, 16, 256), F32), VMEM((8, 256, 128), F32), VMEM((7, 256, 128), F32),
+            VMEM((256, 256), F32), VMEM((256, 256), F32), VMEM((256, 256), F32), VMEM((16, 256), F32), VMEM((8, 16, 256), F32), VMEM((16, 16, 128), F32),
             D((SEMS,)), D((SEMS,)), D((14,)), D((14,)), D((7,)), D((7,)), D((15,)), D((15,)), D((2, 16)), D((2,)), D((2, 8)),
-            D((7,)), D((7,)), D((16,)), D((16,)),
+            D((7,)), D((7,)), D((16,)), D((16,)), D((7,)), D((7,)), D((15,)), D((15,)),
         ],
         compiler_params=pltpu.CompilerParams(has_side_effects=True, vmem_limit_bytes=67043328, collective_id=0),
         name="factor_update",

time: 127 us -> 117 us (0.921)
  Pallas kernels: 124 us -> 115 us
    pallas_call x1, Pallas kernels: 124 us -> 115 us  [main(): pl.pallas_call(main_body, out_shape=(jax.ShapeDtypeStruct((16, 2048), F32...]
where the time goes in v4:
time: 117 us
  Pallas kernels  115 us (98%)
  local copies, waits for them, and re-layouts  1.57 us (1%)
    pallas_call x1, Pallas kernels, main(): pl.pallas_call(main_body, out_shape=(jax.ShapeDtypeStruct((16, 2048), F32...  115 us

profile of v4, /device:TPU:25, one launch (start us, length us, event | category | flops | bytes accessed | tf_op | source)
XLA Modules:
  0.0 116.8 jit_solution(3398362766806152660)
XLA Ops:
  0.7 114.5 %factor_update.1 = (f32[16,2048]{1,0:T(8,128)}, bf16[2,256,256,128]{3,2,1,0:T(8,128)(2,1)}) custom-call(bf16[16,4096]{1,0:T(8,128)(2,1)} %bitcast.6, bf16[16,2048]{1,0:T(8,128)(2,1)} %bitcast.7, s32[512,128]{1,0:T(8,128)} %third_ref.1, bf16[512,128]{1,0:T(8,128)(2,1)} %values_ref.1, s32[512]{0:T(512)} %length_ref.1, s32[1]{0:T(128)S(6)} %copy.10.live_ref, ...), custom_call_target="tpu_custom_call" | custom-call | tf_op jit(solution)/shard_map/factor_update/pallas_call | solution.py:552
  115.2 1.6 %copy.11 = f32[2048,16]{0,1:T(8,128)} copy(f32[2048,16]{0,1:T(8,128)} %bitcast.5) | data formatting | bytes 262144

commit v5 on v4

--- a/solution.py
+++ b/solution.py
@@ -17,7 +17,8 @@
 
 PARTS = ((0, 1152), (1152, 1408), (2560, 1536))
 ORDERS = ("xyz", "yzx", "zxy")
-SEMS = 52 * 3 + 16 * 3
+SENDS = 12
+SEMS = 75
 
 
 def place():
@@ -37,7 +38,6 @@
         self.steps = {d: [me[d], *(lax.rem(me[d] + i, 4) for i in (1, 2, 3))] for d in "zxy"}
         self.other = {**me, "k": 1 - me["k"]}
         self.used = 0
-        self.sent = []
 
     def moved(self, at, dim, step):
         return {**at, dim: self.steps[dim][step]}
@@ -57,25 +57,24 @@
         self.used += 1
         return self.used - 1
 
-    def copy(self, ref, n, to):
-        c = pltpu.make_async_remote_copy(ref, ref, self.send.at[n], self.recv.at[n], device_id=device(to), device_id_type=MESH)
+    def copy(self, ref, n, to, group):
+        c = pltpu.make_async_remote_copy(ref, ref, self.send.at[group], self.recv.at[n], device_id=device(to), device_id_type=MESH)
         c.start()
-        self.sent.append((ref, n))
 
     def arrived(self, ref, n):
-        pltpu.make_async_remote_copy(ref, ref, self.send.at[n], self.recv.at[n], device_id=self.mine, device_id_type=MESH).wait_recv()
+        pltpu.make_async_remote_copy(ref, ref, self.send.at[0], self.recv.at[n], device_id=self.mine, device_id_type=MESH).wait_recv()
 
     def run(self):
         me = self.me
         FORE, BACK = 1, 3
         parts = range(3)
         one = {(p, s): self.new() for p in parts for s in (FORE, BACK)}
-        onef = {(p, s): self.new() for p in parts for s in (FORE, BACK)}
+        onef = {p: self.new() for p in parts}
         two = {(p, o, s): self.new() for p in parts for o in range(4) for s in (FORE, BACK)}
-        twof = {(p, o): self.new() for p in parts for o in range(4)}
-        three = {(p, a, b, s): self.new() for p in parts for a in range(4) for b in range(4) for s in (FORE, BACK)}
+        twof = {p: self.new() for p in parts}
+        three = {(p, b, s): self.new() for p in parts for b in range(4) for s in (FORE, BACK)}
         threef = {(p, o): self.new() for p in parts for o in range(4)}
-        core = {(p, a, b): self.new() for p in parts for a in range(4) for b in range(4)}
+        core = {p: self.new() for p in parts}
 
         def dims(p):
             return ORDERS[p]
@@ -97,18 +96,18 @@
             return self.moved(me, dims(p)[i], s)
 
         def cross(p, b, c):
-            self.copy(set3(p, b, c), core[p, b, c], self.other)
+            self.copy(set3(p, b, c), core[p], self.other, p)
 
         def third(p, a, b):
             for s3 in (FORE, BACK):
-                self.copy(self.block(p, at2(p, a, b)), three[p, a, b, s3], to(p, 2, s3))
+                self.copy(self.block(p, at2(p, a, b)), three[p, b, s3], to(p, 2, s3), p)
 
         for p in parts:
             for s in (FORE, BACK):
-                self.copy(self.block(p, me), one[p, s], to(p, 0, s))
+                self.copy(self.block(p, me), one[p, s], to(p, 0, s), 6 + p)
         for p in parts:
             for s in (FORE, BACK):
-                self.copy(self.block(p, me), two[p, 0, s], to(p, 1, s))
+                self.copy(self.block(p, me), two[p, 0, s], to(p, 1, s), 3 + p)
         for p in parts:
             third(p, 0, 0)
         yield
@@ -116,16 +115,15 @@
             for s in (FORE, BACK):
                 back = 4 - s
                 self.arrived(self.block(p, at1(p, back)), one[p, s])
-                self.copy(self.block(p, at1(p, back), half=0 if s == FORE else 1), onef[p, s], to(p, 0, s))
+                self.copy(self.block(p, at1(p, back), half=0 if s == FORE else 1), onef[p], to(p, 0, s), 9 + p)
                 for s2 in (FORE, BACK):
-                    self.copy(self.block(p, at1(p, back)), two[p, back, s2], to(p, 1, s2))
+                    self.copy(self.block(p, at1(p, back)), two[p, back, s2], to(p, 1, s2), 3 + p)
                 third(p, back, 0)
         yield
         for p in parts:
-            for s in (FORE, BACK):
-                self.arrived(self.block(p, at1(p, 2), half=0 if s == FORE else 1), onef[p, s])
+            self.arrived(self.block(p, at1(p, 2)), onef[p])
             for s2 in (FORE, BACK):
-                self.copy(self.block(p, at1(p, 2)), two[p, 2, s2], to(p, 1, s2))
+                self.copy(self.block(p, at1(p, 2)), two[p, 2, s2], to(p, 1, s2), 3 + p)
             third(p, 2, 0)
             cross(p, 0, 0)
         yield
@@ -136,15 +134,15 @@
                     back = 4 - s
                     self.arrived(self.block(p, at2(p, o, back)), two[p, o, s])
                     if o in FIRST[s]:
-                        self.copy(self.block(p, at2(p, o, back)), twof[p, o], to(p, 1, s))
+                        self.copy(self.block(p, at2(p, o, back)), twof[p], to(p, 1, s), 6 + p)
                     third(p, o, back)
         for p in parts:
             for b in (3, 1):
                 cross(p, b, 0)
         yield
         for p in parts:
+            self.arrived(set3(p, 2, 0), twof[p])
             for o in (0, 3, 1, 2):
-                self.arrived(self.block(p, at2(p, o, 2)), twof[p, o])
                 third(p, o, 2)
             cross(p, 2, 0)
         for b in (0, 3, 1, 2):
@@ -152,10 +150,9 @@
             for p in parts:
                 for s in (FORE, BACK):
                     back = 4 - s
-                    for o in range(4):
-                        self.arrived(self.block(p, self.moved(at2(p, o, b), dims(p)[2], back)), three[p, o, b, s])
+                    self.arrived(set3(p, b, back), three[p, b, s])
                     if b in FIRST[s]:
-                        self.copy(set3(p, b, back), threef[p, b], to(p, 2, s))
+                        self.copy(set3(p, b, back), threef[p, b], to(p, 2, s), 3 + p)
                     cross(p, b, back)
         yield
         for b in (0, 3, 1, 2):
@@ -163,17 +160,17 @@
                 self.arrived(set3(p, b, 2), threef[p, b])
                 cross(p, b, 2)
         for p in parts:
-            for a in range(4):
-                for b in range(4):
-                    self.arrived(set3(p, a, b, k=self.other["k"]), core[p, a, b])
-        for ref, n in self.sent:
-            pltpu.make_async_remote_copy(ref, ref, self.send.at[n], self.recv.at[n], device_id=self.mine, device_id_type=MESH).wait_send()
-
-
-def send_to(src, dst, ssem, rsem, to):
-    c = pltpu.make_async_remote_copy(src, dst, ssem, rsem, device_id=to, device_id_type=MESH)
-    c.start()
-    return c
+            start, size = PARTS[p]
+            lanes = pl.ds(start, size)
+            t = self.t
+            self.arrived(t.at[:, :, self.other["k"], :, :, lanes], core[p])
+            for n, ref in (
+                (p, t.at[0:3, :, :, :, :, lanes]),
+                (3 + p, t.at[0, 0:3, :, :, :, lanes]),
+                (6 + p, t.at[0, 0, :, 0:3, :, lanes]),
+                (9 + p, t.at[0, 0, 0, 0, :, lanes]),
+            ):
+                pltpu.make_async_remote_copy(ref, ref, self.send.at[n], self.recv.at[0], device_id=self.mine, device_id_type=MESH).wait_send()
 
 
 UB = 16
@@ -236,7 +233,7 @@
 
 
 def main_body(piece, spiece, third_ref, values_ref, length_ref, live_ref, sec_ref, own_ref, out, spill,
-              t, s_vm, near, far, part, parts, wfa, wfb, whi, wlo, fold, value_ref, gt_ref, gs_ref, total, got, a_ref, x_ref, r_ref, part3, parts3, answer,
+              t, s_vm, near, far, part, parts, wfa, wfb, whi, wlo, fold, picked, value_ref, gt_ref, gs_ref, total, got, a_ref, x_ref, r_ref, part3, parts3, answer,
               send, recv, ssem, srecv, csem, crecv, gsem, grecv, psem, lsem, lose, rsem, rrecv, xsem, xrecv, csem3, crecv3, gsem3, grecv3):
     r, c = lax.axis_index("rows"), lax.axis_index("cols")
     g = Gather(t, send, recv)
@@ -263,9 +260,8 @@
     pl.semaphore_wait(barrier, 40 - at_home.astype(jnp.int32))
     sent = []
 
-    def push(src, dst, ssem, rsem, n, to):
-        send_to(src, dst, ssem.at[n], rsem.at[n], to)
-        sent.append((lambda: src, ssem, n))
+    def push(src, dst, ssem, rsem, to):
+        send_to(src, dst, ssem, rsem, to)
 
     cp.wait()
     run = g.run()
@@ -328,14 +324,13 @@
         part3[...] = chunk
         parts3[c] = chunk
         for i in range(1, 8):
-            push(part3, parts3.at[c], csem3, crecv3, i - 1, (r, lax.rem(c + i, 8)))
+            push(part3, parts3.at[c], csem3, crecv3, (r, lax.rem(c + i, 8)))
 
     def third_gram_sum():
-        for i in range(1, 8):
-            take(parts3.at[lax.rem(c + 8 - i, 8)], crecv3.at[i - 1], (r, c))
+        take(parts3.at[0:7], crecv3, (r, c))
         gt_ref[r] = sum(parts3[i] for i in range(8))
         for i in range(1, 16):
-            push(mine3, mine3, gsem3, grecv3, i - 1, (lax.rem(r + i, 16), c))
+            push(mine3, mine3, gsem3, grecv3, (lax.rem(r + i, 16), c))
 
     def second_gram():
         for n, z in ((12, 0), (13, 2)):
@@ -344,26 +339,29 @@
         part[...] = chunk
         parts[c] = chunk
         for i in range(1, 8):
-            push(part, parts.at[c], csem, crecv, i - 1, (r, lax.rem(c + i, 8)))
+            push(part, parts.at[c], csem, crecv, (r, lax.rem(c + i, 8)))
 
     def second_gram_sum():
-        for i in range(1, 8):
-            take(parts.at[lax.rem(c + 8 - i, 8)], crecv.at[i - 1], (r, c))
+        take(parts.at[0:7], crecv, (r, c))
         gs_ref[r] = sum(parts[i] for i in range(8))
         for i in range(1, 16):
-            push(mine, mine, gsem, grecv, i - 1, (lax.rem(r + i, 16), c))
+            push(mine, mine, gsem, grecv, (lax.rem(r + i, 16), c))
+
+    def parked(step):
+        both = spill.at[:, :, pl.ds(pl.multiple_of(step * UB, UB), UB), :]
+        pltpu.make_async_copy(both, both, psem.at[step]).wait()
 
     def park(step):
         rows = pl.ds(pl.multiple_of(step * UB, UB), UB)
         return (
-            pltpu.make_async_copy(whi.at[:, rows, :], spill.at[0, :, rows, :], psem.at[0, step]),
-            pltpu.make_async_copy(wlo.at[:, rows, :], spill.at[1, :, rows, :], psem.at[1, step]),
+            pltpu.make_async_copy(whi.at[:, rows, :], spill.at[0, :, rows, :], psem.at[step]),
+            pltpu.make_async_copy(wlo.at[:, rows, :], spill.at[1, :, rows, :], psem.at[step]),
         )
 
     todo = {j: [] for j in range(STEPS // 2)}
     for j in EVENTS:
         todo[j].append(lambda: next(run))
-    for j, f in zip(SECOND_AT, (second_one, second_two, second_three, second_four, second_gram, second_gram_sum)):
+    for j, f in zip(SECOND_AT, (second_one, second_two, second_three, second_four)):
         todo[j].append(f)
 
     def iteration(i, _):
@@ -379,8 +377,7 @@
 
             @pl.when((step >= 16) & (2 * i + half >= 1))
             def _():
-                for x in park(slot):
-                    x.wait()
+                parked(slot)
 
             rows = pl.ds(pl.multiple_of(slot * UB, UB), UB)
             at = pl.multiple_of((2 * i + half) * UB, UB)
@@ -394,18 +391,25 @@
         return 0
 
     lax.fori_loop(0, STEPS // 2, iteration, 0)
-    for x in park(15):
-        x.wait()
+    parked(15)
     for q in range(128):
         split_rows(q, pl.ds(GRP - UB, UB), wfb, whi, wlo)
+    second_gram()
+    one, zero = jnp.ones((), BF), jnp.zeros((), BF)
+    second = jnp.zeros((256, 512), F32)
+    for j in range(4):
+        ij = lax.broadcasted_iota(jnp.int32, (512, 512), 0) + j * 512
+        pick = jnp.where(ij == sec_ref[...] - c * 2048, one, zero)
+        second += lax.dot_general(s_vm[:, :, :, :, j * 512:(j + 1) * 512].reshape(256, 512), pick, NN, preferred_element_type=F32)
+    picked[...] = second
     for _ in run:
         pass
 
     def back(i):
-        tiles = pl.ds(pl.multiple_of(i * 32, 32), 32)
+        tiles = pl.ds(pl.multiple_of(i * 64, 64), 64)
         return (
-            pltpu.make_async_copy(spill.at[0, tiles], whi.at[tiles], lose.at[0, i]),
-            pltpu.make_async_copy(spill.at[1, tiles], wlo.at[tiles], lose.at[1, i]),
+            pltpu.make_async_copy(spill.at[0, tiles], whi.at[tiles], lose.at[i]),
+            pltpu.make_async_copy(spill.at[1, tiles], wlo.at[tiles], lose.at[i]),
         )
 
     third_gram()
@@ -413,11 +417,12 @@
     for first in (True, False):
         def dense(i, _):
             if not first:
-                for x in back(i):
-                    x.wait()
-            y, low = lax.div(i, 2), lax.rem(i, 2)
-            tt = jnp.concatenate([t[low + 2 * h, :, :, y].reshape(128, 4096) for h in range(2)], 0)
-            side = lambda w: jnp.concatenate([w[i * 32 + j] for j in range(32)], 1)
+                both = spill.at[:, pl.ds(pl.multiple_of(i * 64, 64), 64)]
+                pltpu.make_async_copy(both, both, lose.at[i]).wait()
+            tt = jnp.concatenate(
+                [jnp.concatenate([t[low + 2 * h, :, :, i].reshape(128, 4096) for h in range(2)], 0) for low in range(2)], 1
+            )
+            side = lambda w: jnp.concatenate([w[i * 64 + j] for j in range(64)], 1)
             lhs = jnp.concatenate([side(whi), side(wlo)], 0)
             res = lax.dot_general(lhs, tt, NT, preferred_element_type=F32)
             fold[pl.ds(GRP if first else 0, GRP), :] += res[:GRP] + res[GRP:]
@@ -426,17 +431,12 @@
                     x.start()
             return 0
 
-        lax.fori_loop(0, 8, dense, 0)
+        lax.fori_loop(0, 4, dense, 0)
         if first:
+            second_gram_sum()
             third_gram_sum()
 
-    one, zero = jnp.ones((), BF), jnp.zeros((), BF)
-    second = jnp.zeros((256, 512), F32)
-    for j in range(4):
-        ij = lax.broadcasted_iota(jnp.int32, (512, 512), 0) + j * 512
-        pick = jnp.where(ij == sec_ref[...] - c * 2048, one, zero)
-        second += lax.dot_general(s_vm[:, :, :, :, j * 512:(j + 1) * 512].reshape(256, 512), pick, NN, preferred_element_type=F32)
-    contrib = second * fold[...].T
+    contrib = picked[...] * fold[...].T
     hi = contrib.astype(BF)
     lhs = jnp.concatenate([hi, (contrib - hi.astype(F32)).astype(BF)], 0)
     for j in range(4):
@@ -448,15 +448,14 @@
             total[2 * j + h] = both[:, h * 128:(h + 1) * 128]
     for i in range(1, 8):
         to = lax.rem(c + i, 8)
-        send_to(total.at[to], got.at[i - 1], rsem.at[i - 1], rrecv.at[i - 1], (r, to))
-
-    for i in range(1, 16):
-        take(gs_ref.at[lax.rem(r + 16 - i, 16)], grecv.at[i - 1], (r, c))
-        take(gt_ref.at[lax.rem(r + 16 - i, 16)], grecv3.at[i - 1], (r, c))
+        send_to(total.at[to], got.at[i - 1], rsem, rrecv, (r, to))
+
+    take(gs_ref.at[0:15], grecv, (r, c))
+    take(gt_ref.at[0:15], grecv3, (r, c))
     invert(gs_ref, gt_ref, a_ref, x_ref, r_ref)
     rows = total[c]
+    take(got, rrecv, (r, c))
     for i in range(7):
-        take(got.at[i], rrecv.at[i], (r, c))
         rows = rows + got[i]
     answer[...] = lax.dot_general(a_ref[...], rows, NN, precision=HIGH, preferred_element_type=F32).reshape(16, 16, 128)
 
@@ -464,9 +463,9 @@
     lanes = pl.ds(pl.multiple_of(slot * 128, 128), 128)
     for i in range(1, 16):
         to = lax.rem(r + i, 16)
-        send_to(answer.at[to], out.at[:, lanes], xsem.at[i], xrecv.at[slot], (to, home))
+        send_to(answer.at[to], out.at[:, lanes], xsem, xrecv, (to, home))
     here = pltpu.make_async_copy(answer.at[r], out.at[:, lanes], lsem.at[0])
-    away = pltpu.make_async_remote_copy(answer.at[r], out.at[:, lanes], xsem.at[0], xrecv.at[slot], device_id=(r, home), device_id_type=MESH)
+    away = pltpu.make_async_remote_copy(answer.at[r], out.at[:, lanes], xsem, xrecv, device_id=(r, home), device_id_type=MESH)
 
     @pl.when(at_home)
     def _():
@@ -479,25 +478,25 @@
     for make, sem, n in sent:
         ref = make()
         pltpu.make_async_remote_copy(ref, ref, sem.at[n], sem.at[n], device_id=(r, c), device_id_type=MESH).wait_send()
-    for i in range(1, 8):
-        pltpu.make_async_remote_copy(got.at[i - 1], got.at[i - 1], rsem.at[i - 1], rrecv.at[i - 1], device_id=(r, c), device_id_type=MESH).wait_send()
-    for i in range(16):
-        there = out.at[:, pl.ds(i * 128, 128)]
-
-        @pl.when(jnp.logical_not(at_home & (slot == i)))
-        def _():
-            take(there, xrecv.at[i], (r, c))
+    def all_sent(ref, sem):
+        pltpu.make_async_remote_copy(ref, ref, sem, sem, device_id=(r, c), device_id_type=MESH).wait_send()
+
+    all_sent(got, rsem)
+    all_sent(parts.at[0:7], csem)
+    all_sent(parts3.at[0:7], csem3)
+    all_sent(gs_ref.at[0:15], gsem)
+    all_sent(gt_ref.at[0:15], gsem3)
 
     @pl.when(at_home)
     def _():
+        take(out.at[:, 0:1920], xrecv, (r, c))
         here.wait()
+        all_sent(answer.at[0:15], xsem)
 
     @pl.when(jnp.logical_not(at_home))
     def _():
-        away.wait_send()
-
-    for i in range(1, 16):
-        pltpu.make_async_remote_copy(answer.at[0], answer.at[0], xsem.at[i], xrecv.at[0], device_id=(r, c), device_id_type=MESH).wait_send()
+        take(out, xrecv, (r, c))
+        all_sent(answer, xsem)
 
 
 def invert(gs_ref, gt_ref, a_ref, x_ref, r_ref):
@@ -543,7 +542,7 @@
 
 DOUBLINGS = 20
 EVENTS = (1, 3, 5, 7, 9, 11, 13, 15)
-SECOND_AT = (1, 3, 5, 8, 10, 14)
+SECOND_AT = (1, 3, 10, 15)
 
 
 def main(piece, spiece, third, values, length, live, sec, own):
@@ -558,11 +557,10 @@
             VMEM((4, 4, 2, 4, 16, 4096), BF), VMEM((2, 4, 2, 16, 2048), BF), VMEM((2, 16, 2048), BF), VMEM((2, 16, 2048), BF),
             VMEM((16, 256), F32), VMEM((8, 16, 256), F32),
             VMEM((2, UB * PAD, 128), F32), VMEM((2, UB * PAD, 128), F32),
-            VMEM((256, GRP, 128), BF), VMEM((256, GRP, 128), BF), VMEM((512, 256), F32), VMEM((512, 128), F32),
+            VMEM((256, GRP, 128), BF), VMEM((256, GRP, 128), BF), VMEM((512, 256), F32), VMEM((256, 512), F32), VMEM((512, 128), F32),
             VMEM((16, 16, 256), F32), VMEM((16, 16, 256), F32), VMEM((8, 256, 128), F32), VMEM((7, 256, 128), F32),
             VMEM((256, 256), F32), VMEM((256, 256), F32), VMEM((256, 256), F32), VMEM((16, 256), F32), VMEM((8, 16, 256), F32), VMEM((16, 16, 128), F32),
-            D((SEMS,)), D((SEMS,)), D((14,)), D((14,)), D((7,)), D((7,)), D((15,)), D((15,)), D((2, 16)), D((2,)), D((2, 8)),
-            D((7,)), D((7,)), D((16,)), D((16,)), D((7,)), D((7,)), D((15,)), D((15,)),
+            D((SENDS,)), D((SEMS,)), D((14,)), D((14,)), *[D(())] * 4, D((16,)), D((2,)), D((4,)), *[D(())] * 8,
         ],
         compiler_params=pltpu.CompilerParams(has_side_effects=True, vmem_limit_bytes=67043328, collective_id=0),
         name="factor_update",

time: 117 us -> 106 us (0.906)
  Pallas kernels: 115 us -> 104 us
    pallas_call x1, Pallas kernels: 115 us -> 104 us  [main(): pl.pallas_call(main_body, out_shape=(jax.ShapeDtypeStruct((16, 2048), F32...]
where the time goes in v5:
time: 106 us
  Pallas kernels  104 us (98%)
  local copies, waits for them, and re-layouts  1.57 us (1%)
    pallas_call x1, Pallas kernels, main(): pl.pallas_call(main_body, out_shape=(jax.ShapeDtypeStruct((16, 2048), F32...  104 us

profile of v5, /device:TPU:25, one launch (start us, length us, event | category | flops | bytes accessed | tf_op | source)
XLA Modules:
  0.0 106.1 jit_solution(4034568048960673619)
XLA Ops:
  0.7 103.9 %factor_update.1 = (f32[16,2048]{1,0:T(8,128)}, bf16[2,256,256,128]{3,2,1,0:T(8,128)(2,1)}) custom-call(bf16[16,4096]{1,0:T(8,128)(2,1)} %bitcast.6, bf16[16,2048]{1,0:T(8,128)(2,1)} %bitcast.7, s32[512,128]{1,0:T(8,128)} %third_ref.1, bf16[512,128]{1,0:T(8,128)(2,1)} %values_ref.1, s32[512]{0:T(512)} %length_ref.1, s32[1]{0:T(128)S(6)} %copy.10.live_ref, ...), custom_call_target="tpu_custom_call" | custom-call | tf_op jit(solution)/shard_map/factor_update/pallas_call | solution.py:551
  104.6 1.6 %copy.11 = f32[2048,16]{0,1:T(8,128)} copy(f32[2048,16]{0,1:T(8,128)} %bitcast.5) | data formatting | bytes 262144

commit v6 on v5

--- a/solution.py
+++ b/solution.py
@@ -232,8 +232,8 @@
     pltpu.make_async_remote_copy(ref, ref, sem, sem, device_id=me, device_id_type=MESH).wait_recv()
 
 
-def main_body(piece, spiece, third_ref, values_ref, length_ref, live_ref, sec_ref, own_ref, out, spill,
-              t, s_vm, near, far, part, parts, wfa, wfb, whi, wlo, fold, picked, value_ref, gt_ref, gs_ref, total, got, a_ref, x_ref, r_ref, part3, parts3, answer,
+def main_body(piece, spiece, third_ref, values_ref, length_ref, live_hbm, sec_ref, own_ref, out, spill,
+              t, s_vm, near, far, part, parts, wfa, wfb, whi, wlo, fold, picked, value_ref, live_ref, gt_ref, gs_ref, total, got, a_ref, x_ref, r_ref, part3, parts3, answer,
               send, recv, ssem, srecv, csem, crecv, gsem, grecv, psem, lsem, lose, rsem, rrecv, xsem, xrecv, csem3, crecv3, gsem3, grecv3):
     r, c = lax.axis_index("rows"), lax.axis_index("cols")
     g = Gather(t, send, recv)
@@ -242,22 +242,17 @@
     cp.start()
     cs = pltpu.make_async_copy(spiece, s_vm.at[lax.div(me["z"], 2), me["x"], me["k"]], lsem.at[1])
     cs.start()
-    peers = [(lax.rem(r + i, 16), c) for i in range(1, 16)] + [(r, lax.rem(c + i, 8)) for i in range(1, 8)]
-    peers += [device(g.moved(me, "z", 1)), device(g.moved(me, "z", 3))]
-    barrier = pltpu.get_barrier_semaphore()
-    for to in peers:
-        pl.semaphore_signal(barrier, inc=1, device_id=to, device_id_type=MESH)
     home = lax.div(r, 2)
     at_home = home == c
-    for i in range(16):
-        source = (2 * c + i // 8, i % 8)
-
-        @pl.when(jnp.logical_not((source[0] == r) & (c == source[1])))
-        def _():
-            pl.semaphore_signal(barrier, inc=1, device_id=source, device_id_type=MESH)
+    barrier = pltpu.get_barrier_semaphore()
+    for to in [device(g.moved(me, d, way)) for d in "xyz" for way in (1, 3)] + [device(g.other)]:
+        pl.semaphore_signal(barrier, inc=1, device_id=to, device_id_type=MESH)
+    cl = pltpu.make_async_copy(live_hbm, live_ref, lsem.at[2])
+    cl.start()
+    cl.wait()
     value_ref[...] = values_ref[...].astype(F32)
     ins = (third_ref, value_ref, length_ref, live_ref)
-    pl.semaphore_wait(barrier, 40 - at_home.astype(jnp.int32))
+    pl.semaphore_wait(barrier, 7)
     sent = []
 
     def push(src, dst, ssem, rsem, to):
@@ -446,9 +441,10 @@
         both = res[:256] + res[256:]
         for h in range(2):
             total[2 * j + h] = both[:, h * 128:(h + 1) * 128]
-    for i in range(1, 8):
-        to = lax.rem(c + i, 8)
-        send_to(total.at[to], got.at[i - 1], rsem, rrecv, (r, to))
+        for to in (2 * j, 2 * j + 1):
+            @pl.when(c != to)
+            def _():
+                send_to(total.at[to], got.at[lax.rem(to - c + 8, 8) - 1], rsem, rrecv, (r, to))
 
     take(gs_ref.at[0:15], grecv, (r, c))
     take(gt_ref.at[0:15], grecv3, (r, c))
@@ -551,16 +547,16 @@
     return pl.pallas_call(
         main_body,
         out_shape=(jax.ShapeDtypeStruct((16, 2048), F32), jax.ShapeDtypeStruct((2, 256, GRP, 128), BF)),
-        in_specs=[ANY, ANY, INV, INV, smem, smem, INV, INV],
+        in_specs=[ANY, ANY, INV, INV, smem, ANY, INV, INV],
         out_specs=(INV, ANY),
         scratch_shapes=[
             VMEM((4, 4, 2, 4, 16, 4096), BF), VMEM((2, 4, 2, 16, 2048), BF), VMEM((2, 16, 2048), BF), VMEM((2, 16, 2048), BF),
             VMEM((16, 256), F32), VMEM((8, 16, 256), F32),
             VMEM((2, UB * PAD, 128), F32), VMEM((2, UB * PAD, 128), F32),
-            VMEM((256, GRP, 128), BF), VMEM((256, GRP, 128), BF), VMEM((512, 256), F32), VMEM((256, 512), F32), VMEM((512, 128), F32),
+            VMEM((256, GRP, 128), BF), VMEM((256, GRP, 128), BF), VMEM((512, 256), F32), VMEM((256, 512), F32), VMEM((512, 128), F32), pltpu.SMEM((1,), jnp.int32),
             VMEM((16, 16, 256), F32), VMEM((16, 16, 256), F32), VMEM((8, 256, 128), F32), VMEM((7, 256, 128), F32),
             VMEM((256, 256), F32), VMEM((256, 256), F32), VMEM((256, 256), F32), VMEM((16, 256), F32), VMEM((8, 16, 256), F32), VMEM((16, 16, 128), F32),
-            D((SENDS,)), D((SEMS,)), D((14,)), D((14,)), *[D(())] * 4, D((16,)), D((2,)), D((4,)), *[D(())] * 8,
+            D((SENDS,)), D((SEMS,)), D((14,)), D((14,)), *[D(())] * 4, D((16,)), D((3,)), D((4,)), *[D(())] * 8,
         ],
         compiler_params=pltpu.CompilerParams(has_side_effects=True, vmem_limit_bytes=67043328, collective_id=0),
         name="factor_update",

time: 106 us -> 104 us (0.981)
  Pallas kernels: 104 us -> 102 us
    pallas_call x1, Pallas kernels: 104 us -> 102 us  [main(): pl.pallas_call(main_body, out_shape=(jax.ShapeDtypeStruct((16, 2048), F32...]
where the time goes in v6:
time: 104 us
  Pallas kernels  102 us (98%)
  local copies, waits for them, and re-layouts  1.57 us (2%)
    pallas_call x1, Pallas kernels, main(): pl.pallas_call(main_body, out_shape=(jax.ShapeDtypeStruct((16, 2048), F32...  102 us

profile of v6, /device:TPU:25, one launch (start us, length us, event | category | flops | bytes accessed | tf_op | source)
XLA Modules:
  0.0 103.8 jit_solution(1718897006912990594)
XLA Ops:
  0.7 101.6 %factor_update.1 = (f32[16,2048]{1,0:T(8,128)}, bf16[2,256,256,128]{3,2,1,0:T(8,128)(2,1)}) custom-call(bf16[16,4096]{1,0:T(8,128)(2,1)} %bitcast.6, bf16[16,2048]{1,0:T(8,128)(2,1)} %bitcast.7, s32[512,128]{1,0:T(8,128)} %third_ref.1, bf16[512,128]{1,0:T(8,128)(2,1)} %values_ref.1, s32[512]{0:T(512)} %length_ref.1, s32[1]{0:T(128)S(6)} %copy.10.live_hbm, ...), custom_call_target="tpu_custom_call" | custom-call | tf_op jit(solution)/shard_map/factor_update/pallas_call | solution.py:547
  102.2 1.6 %copy.11 = f32[2048,16]{0,1:T(8,128)} copy(f32[2048,16]{0,1:T(8,128)} %bitcast.5) | data formatting | bytes 262144

commit v7 on v6

--- a/solution.py
+++ b/solution.py
@@ -434,14 +434,17 @@
     contrib = picked[...] * fold[...].T
     hi = contrib.astype(BF)
     lhs = jnp.concatenate([hi, (contrib - hi.astype(F32)).astype(BF)], 0)
-    for j in range(4):
+    for turn in range(4):
+        j = lax.rem(lax.div(c, 2) + 1 + turn, 4)
         ii = lax.broadcasted_iota(jnp.int32, (256, 512), 0) + j * 256
         put = jnp.where(ii == own_ref[...] - r * 1024, one, zero)
         res = lax.dot_general(lhs, put, NT, preferred_element_type=F32)
         both = res[:256] + res[256:]
         for h in range(2):
             total[2 * j + h] = both[:, h * 128:(h + 1) * 128]
-        for to in (2 * j, 2 * j + 1):
+        for h in range(2):
+            to = 2 * j + h
+
             @pl.when(c != to)
             def _():
                 send_to(total.at[to], got.at[lax.rem(to - c + 8, 8) - 1], rsem, rrecv, (r, to))

time: 104 us -> 102 us (0.981)
  Pallas kernels: 102 us -> 99.1 us
    pallas_call x1, Pallas kernels: 102 us -> 99.1 us  [main(): pl.pallas_call(main_body, out_shape=(jax.ShapeDtypeStruct((16, 2048), F32...]
where the time goes in v7:
time: 102 us; the launch traced here: 101 us
  Pallas kernels  99.1 us (97%)
  local copies, waits for them, and re-layouts  1.57 us (2%)
    pallas_call x1, Pallas kernels, main(): pl.pallas_call(main_body, out_shape=(jax.ShapeDtypeStruct((16, 2048), F32...  99.1 us

profile of v7, /device:TPU:25, one launch (start us, length us, event | category | flops | bytes accessed | tf_op | source)
XLA Modules:
  0.0 101.3 jit_solution(6126492312617233730)
XLA Ops:
  0.7 99.1 %factor_update.1 = (f32[16,2048]{1,0:T(8,128)}, bf16[2,256,256,128]{3,2,1,0:T(8,128)(2,1)}) custom-call(bf16[16,4096]{1,0:T(8,128)(2,1)} %bitcast.6, bf16[16,2048]{1,0:T(8,128)(2,1)} %bitcast.7, s32[512,128]{1,0:T(8,128)} %third_ref.1, bf16[512,128]{1,0:T(8,128)(2,1)} %values_ref.1, s32[512]{0:T(512)} %length_ref.1, s32[1]{0:T(128)S(6)} %copy.10.live_hbm, ...), custom_call_target="tpu_custom_call" | custom-call | tf_op jit(solution)/shard_map/factor_update/pallas_call | solution.py:550
  99.7 1.6 %copy.11 = f32[2048,16]{0,1:T(8,128)} copy(f32[2048,16]{0,1:T(8,128)} %bitcast.5) | data formatting | bytes 262144
